TPU v7x, 512 devices: a whole 4x4x16 slice. The times are simulated.
512 devices in a mesh: dp: 32 (over y, z_lo, core), mp: 16 (over x, z_hi).
Axes of the slice: x: 4, y: 4, z: 16 (z_hi: 4, z_lo: 4; z = z_hi * 4 + z_lo), core: 2. Of those that a mesh axis runs over, the one named last changes fastest.
Arguments:
- token_ids: int32 [64], replicated, may hold values from 0 to 49151
- cache_lengths: int32 [64], P('dp'), may hold values from 1 to 512
- embedding: bfloat16 [49152, 12288], P(('dp', 'mp')), may hold values from -6 to 6
- ln_gain: float32 [12288], replicated, may hold values from 0.25 to 1.75
- query_weight: bfloat16 [12288, 6144], P('dp', 'mp'), may hold values from -0.0546875 to 0.0546875
- key_cache: bfloat16 [64, 512, 6144], P('dp', None, 'mp'), may hold values from -1000 to 1000
- value_cache: bfloat16 [64, 512, 6144], P('dp', None, 'mp'), may hold values from -6 to 6
- out_weight: bfloat16 [6144, 12288], P('mp', 'dp'), may hold values from -0.078125 to 0.078125
- final_gain: float32 [12288], replicated, may hold values from 0.25 to 1.75
Outputs:
- log_probs: float32 [64, 49152], P(None, ('dp', 'mp'))
All inputs are finite; a program needn't handle non-finite values.
Results may differ from a plain program's by a relative error of at most 0.00033.
Values may be sent and summed in bfloat16 or wider, within the bound.
A program may use at most 64 MiB of HBM per device.

v0:
```python
import jax
import jax.numpy as jnp
from jax import lax
from jax.sharding import Mesh
from jax.sharding import PartitionSpec as P

HD = 128
DP_MP = ("dp_0", "dp_1", "dp_2", "mp_0", "mp_1")
DP = ("dp_0", "dp_1", "dp_2")
MP = ("mp_0", "mp_1")


def split_up(x, dim, devices):
    shape = x.shape
    tiles = x.reshape(*shape[:dim], devices, shape[dim] // devices, *shape[dim + 1 :])
    return jnp.moveaxis(tiles, dim, 0)


def sent_and_summed(x, axis, dim):
    devices = lax.axis_size(axis)
    tiles = lax.all_to_all(split_up(x, dim, devices), axis, 0, 0, tiled=True)
    return jnp.sum(tiles.astype(jnp.float32), axis=0)


def sum_by_axis(x, axes, dim):
    far, near = axes
    own = sent_and_summed(split_up(x, dim, lax.axis_size(far)), near, dim + 1)
    return jnp.sum(
        lax.all_to_all(own.astype(jnp.bfloat16), far, 0, 0, tiled=True).astype(jnp.float32), axis=0
    )


def total_of_pieces(x, axis):
    tiles = lax.all_gather(x, axis).astype(jnp.float32)
    return tiles.sum(axis=0)


def from_everyone(x, axis):
    copies = jnp.broadcast_to(x, (lax.axis_size(axis), *x.shape))
    return lax.all_to_all(copies, axis, split_axis=0, concat_axis=0, tiled=True)


def of_everyone(x, axis):
    return from_everyone(x, axis).sum(axis=0)


def packed_total(arrays, axis):
    line, at, finished = (jnp.concatenate([a.reshape(-1) for a in arrays]), 0, [])
    running = of_everyone(line, axis)
    for a in arrays:
        finished.append(running[at : at + a.size].reshape(a.shape))
        at += a.size
    return tuple(finished)


def joined_along(tiles, dim):
    shape = list(tiles.shape[1:])
    shape[dim] *= tiles.shape[0]
    return jnp.moveaxis(tiles, 0, dim).reshape(shape)


def gather_directly(x, axis, dim):
    return joined_along(from_everyone(x, axis), dim)


def over_pieces(x, axis):
    tiles = lax.all_gather(x, axis)
    return tiles.sum(axis=0)


def whole_of(x, axes, dim):
    far, near = axes
    tiles = from_everyone(from_everyone(x, far), near)
    return joined_along(tiles.swapaxes(0, 1).reshape(-1, *x.shape), dim)


def all_in_one(x, axis):
    leaves = jax.tree.leaves(x)
    sequence = sorted(range(len(leaves)), key=lambda k: -leaves[k].size)
    width = (1, *leaves[sequence[0]].shape)[-1]
    lines = [
        jnp.pad(leaves[k].reshape(-1), (0, -leaves[k].size % width)).reshape(-1, width)
        for k in sequence
    ]
    both, at, found = (lax.all_gather(jnp.concatenate(lines), axis), 0, {})
    for k, line in zip(sequence, lines):
        share = both[:, at : at + len(line)].reshape(len(both), -1)
        found[k] = share[:, : leaves[k].size].reshape(-1, *leaves[k].shape)
        at += len(line)
    numbers = iter(range(len(leaves)))
    return jax.tree.map(lambda _: found[next(numbers)], x)


def joined_all(x, axes, combine):
    for axis in axes:
        pieces = all_in_one(x, axis)
        x = jax.tree.map(lambda part: part[0], pieces)
        for k in range(1, lax.axis_size(axis)):
            x = combine(x, jax.tree.map(lambda part: part[k], pieces))
    return x


def combine_stats(earlier, later):
    row_top = jnp.maximum(earlier[0], later[0])
    summed = earlier[1] * jnp.exp(earlier[0] - row_top) + later[1] * jnp.exp(later[0] - row_top)
    return (row_top, summed)


def per_device(
    token_ids,
    cache_lengths,
    embedding,
    ln_gain,
    query_weight,
    key_cache,
    value_cache,
    out_weight,
    final_gain,
):
    voc_rows = embedding.shape[0]
    model_width = embedding.shape[1]
    vocab_start = lax.axis_index(DP_MP) * voc_rows
    one_hot = (token_ids[:, None] - vocab_start == jnp.arange(voc_rows)[None, :]).astype(
        jnp.bfloat16
    )
    partial_rows = jnp.dot(one_hot, embedding, preferred_element_type=jnp.float32)
    seq_here = key_cache.shape[0]
    cache_len = key_cache.shape[1]
    cols_here = out_weight.shape[1]
    dp_index = lax.axis_index(DP)
    block_sums = sum_by_axis(partial_rows.astype(jnp.bfloat16), (("dp_0", "dp_1"), "dp_2"), 1)
    embedded_cols = total_of_pieces(block_sums.astype(jnp.bfloat16), MP).astype(jnp.float32)
    first_sum, first_sq = packed_total(
        (jnp.sum(embedded_cols, axis=-1), jnp.sum(embedded_cols * embedded_cols, axis=-1)), DP
    )
    first_mean = first_sum / model_width
    first_var = first_sq / model_width - first_mean * first_mean
    ln_here = lax.dynamic_slice_in_dim(ln_gain, dp_index * cols_here, cols_here, 0)
    normed_cols = (
        ln_here * (embedded_cols - first_mean[:, None]) * lax.rsqrt(first_var[:, None] + 1e-05)
    ).astype(jnp.bfloat16)
    own_rows = lax.all_to_all(normed_cols, DP, split_axis=0, concat_axis=1, tiled=True)
    query_sum = jnp.dot(
        own_rows,
        lax.all_gather(query_weight, DP, axis=0, tiled=True),
        preferred_element_type=jnp.float32,
    )
    queries = (query_sum * HD ** (-0.5)).astype(jnp.bfloat16)
    heads_here = queries.shape[1] // HD
    head_query = queries.reshape(seq_here, heads_here, HD)
    key_heads = key_cache.reshape(seq_here, cache_len, heads_here, HD)
    value_heads = value_cache.reshape(seq_here, cache_len, heads_here, HD)
    scores = jnp.einsum("shd,sthd->sht", head_query, key_heads, preferred_element_type=jnp.float32)
    live_mask = jnp.arange(cache_len)[None, None, :] < cache_lengths[:, None, None]
    scores = jnp.where(live_mask, scores, jnp.float32(-1e30))
    row_top = jnp.max(scores, axis=-1, keepdims=True)
    exp_terms = jnp.exp(scores - row_top)
    weights = (exp_terms / jnp.sum(exp_terms, axis=-1, keepdims=True)).astype(jnp.bfloat16)
    attended = jnp.einsum("sht,sthd->shd", weights, value_heads, preferred_element_type=jnp.float32)
    attended = attended.astype(jnp.bfloat16).reshape(seq_here, heads_here * HD)
    every_seq = gather_directly(attended, DP, 0)
    mixed_out = over_pieces(jnp.dot(every_seq, out_weight, preferred_element_type=jnp.float32), MP)
    hidden = embedded_cols + mixed_out
    row_sum, row_sq = packed_total(
        (jnp.sum(hidden, axis=-1), jnp.sum(hidden * hidden, axis=-1)), DP
    )
    row_mean = row_sum / model_width
    row_var = row_sq / model_width - row_mean * row_mean
    gain_here = lax.dynamic_slice_in_dim(final_gain, dp_index * cols_here, cols_here, 0)
    final_normed = (
        gain_here * (hidden - row_mean[:, None]) * lax.rsqrt(row_var[:, None] + 1e-05)
    ).astype(jnp.bfloat16)
    logits = lax.dot_general(
        whole_of(final_normed, (("dp_0", "dp_1"), "dp_2"), 1),
        embedding,
        (((1,), (1,)), ((), ())),
        preferred_element_type=jnp.float32,
    )
    local_top = jnp.max(logits, axis=-1)
    local_exp = jnp.sum(jnp.exp(logits - local_top[:, None]), axis=-1)
    global_top, total_exp = joined_all((local_top, local_exp), DP_MP, combine_stats)
    return logits - global_top[:, None] - jnp.log(total_exp)[:, None]


def solution(mesh):
    finer = Mesh(mesh.devices.reshape(4, 4, 2, 4, 4), ("dp_0", "dp_1", "dp_2", "mp_0", "mp_1"))
    placed = (
        P(),
        P(DP),
        P(DP_MP, None),
        P(),
        P(DP, MP),
        P(DP, None, MP),
        P(DP, None, MP),
        P(MP, DP),
        P(),
    )
    return jax.shard_map(
        per_device, mesh=finer, in_specs=placed, out_specs=P(None, DP_MP), check_vma=False
    )
```

profile of v0, /device:TPU:1, one launch (start us, length us, event | category | flops | bytes accessed | tf_op | source)
XLA Modules:
  0.0 356.0 jit_solution(14191205691028106227)
XLA Ops:
  10.2 4.4 %reshape.862 = bf16[16,64,2,384]{3,2,1,0:T(2,128)(2,1)} reshape(bf16[16,64,768]{2,1,0:T(8,128)(2,1)} %bitcast.391) | data formatting | bytes 3145728 | tf_op jit(solution)/shard_map/reshape | solution.py:15
  14.5 2.3 copy.42
  16.9 12.3 %all_to_all.53 = bf16[2,16,64,384]{3,1,2,0:T(8,128)(2,1)} all-to-all(bf16[2,16,64,384]{3,1,2,0:T(8,128)(2,1)S(1)} %copy.42), channel_id=1, replica_groups=mesh['dp_0'=4,'dp_1'=4,'dp_2'=2,'mp_0'=4,'mp_1'=4] {'dp_2'}, dimensions={0} | all-to-all | bytes 3145728 | tf_op jit(solution)/shard_map/all_to_all | solution.py:21
  29.2 2.1 reduce_sum.116
  31.5 28.3 %all_to_all.54 = bf16[16,64,384]{2,1,0:T(8,128)(2,1)S(1)} all-to-all(bf16[16,64,384]{2,1,0:T(8,128)(2,1)S(1)} %copy.44), channel_id=1, replica_groups=mesh['dp_0'=4,'dp_1'=4,'dp_2'=2,'mp_0'=4,'mp_1'=4] {'dp_0','dp_1'}, dimensions={0} | all-to-all | bytes 1572864 | tf_op jit(solution)/shard_map/all_to_all | solution.py:29
  59.9 64.6 %all-gather = bf16[1024,384]{1,0:T(8,128)(2,1)S(1)} all-gather(bf16[64,384]{1,0:T(8,128)(2,1)S(1)} %reduce_sum.117), channel_id=2, replica_groups=mesh['dp_0'=4,'dp_1'=4,'dp_2'=2,'mp_0'=4,'mp_1'=4] {'mp_0','mp_1'}, dimensions={0}, use_global_device_ids=true | all-gather | bytes 835584 | tf_op jit(solution)/shard_map/all_gather | solution.py:34
  125.8 19.5 %all-to-all-start.2 = ((f32[32,1,128]{2,1,0:T(1,128)}), f32[32,1,128]{2,1,0:T(1,128)S(1)}, u32[]{:S(2)}, u32[]{:S(2)}) async-start(f32[32,1,128]{2,1,0:T(1,128)} %broadcast_in_dim.23), calls=%async_computation.2 | async-start | bytes 32768 | tf_op jit(solution)/shard_map/all_to_all | solution.py:40
  145.3 2.3 copy.46
  149.8 2.6 all-to-all-done.2
  153.5 5.1 %all-to-all-start.3 = ((bf16[32,2,384]{2,1,0:T(2,128)(2,1)}), bf16[32,2,384]{2,1,0:T(2,128)(2,1)S(1)}, u32[]{:S(2)}, u32[]{:S(2)}) async-start(bf16[32,2,384]{2,1,0:T(2,128)(2,1)} %multiply_convert_fusion.1), calls=%async_computation.3 | async-start | bytes 98304 | tf_op jit(solution)/shard_map/all_to_all | solution.py:142
  158.7 7.5 %all-to-all-done.3 = bf16[32,2,384]{2,1,0:T(2,128)(2,1)S(1)} async-done(((bf16[32,2,384]{2,1,0:T(2,128)(2,1)}), bf16[32,2,384]{2,1,0:T(2,128)(2,1)S(1)}, u32[]{:S(2)}, u32[]{:S(2)}) %all-to-all-start.3) | async-done | bytes 49184 | tf_op jit(solution)/shard_map/all_to_all | solution.py:142
  166.3 5.0 %fusion.7 = bf16[2,384]{1,0:T(2,128)(2,1)S(1)} fusion(bf16[2,12288]{1,0:T(2,128)(2,1)S(1)} %bitcast.398, bf16[12288,384]{1,0:T(8,128)(2,1)} %all-gather.15.cloned.1.call-done), kind=kOutput, calls=%fused_computation.10 | convolution fusion | flops 18875904 | bytes 9487872 | tf_op jit(solution)/shard_map/dot_general | solution.py:143
  171.3 2.0 fusion.74
  174.5 10.9 %all_to_all.55 = bf16[32,2,384]{2,1,0:T(2,128)(2,1)S(1)} all-to-all(bf16[32,2,384]{2,1,0:T(2,128)(2,1)S(1)} %broadcast_in_dim.25), channel_id=1, replica_groups=mesh['dp_0'=4,'dp_1'=4,'dp_2'=2,'mp_0'=4,'mp_1'=4] {'dp_0','dp_1','dp_2'}, dimensions={0} | all-to-all | bytes 98304 | tf_op jit(solution)/shard_map/all_to_all | solution.py:40
  186.3 75.8 %all-gather.17.cloned.1.call-done = f32[1024,384]{1,0:T(8,128)} async-done(((f32[64,384]{1,0:T(8,128)}), f32[1024,384]{1,0:T(8,128)}) %all-gather.17.cloned.1.call-update) | async-done | bytes 1572880 | tf_op jit(solution)/shard_map/all_gather | solution.py:67
  264.4 7.3 %all-to-all-start.5 = ((f32[32,1,128]{2,1,0:T(1,128)}), f32[32,1,128]{2,1,0:T(1,128)S(1)}, u32[]{:S(2)}, u32[]{:S(2)}) async-start(f32[32,1,128]{2,1,0:T(1,128)} %broadcast_in_dim.26), calls=%async_computation.5 | async-start | bytes 32768 | tf_op jit(solution)/shard_map/all_to_all | solution.py:40
  272.5 6.4 %all-to-all-done.5 = f32[32,1,128]{2,1,0:T(1,128)S(1)} async-done(((f32[32,1,128]{2,1,0:T(1,128)}), f32[32,1,128]{2,1,0:T(1,128)S(1)}, u32[]{:S(2)}, u32[]{:S(2)}) %all-to-all-start.5) | async-done | bytes 16416 | tf_op jit(solution)/shard_map/all_to_all | solution.py:40
  279.1 24.1 %all_to_all.56 = bf16[16,64,384]{2,1,0:T(8,128)(2,1)S(1)} all-to-all(bf16[16,64,384]{2,1,0:T(8,128)(2,1)S(1)} %broadcast_in_dim.27), channel_id=1, replica_groups=mesh['dp_0'=4,'dp_1'=4,'dp_2'=2,'mp_0'=4,'mp_1'=4] {'dp_0','dp_1'}, dimensions={0} | all-to-all | bytes 1572864 | tf_op jit(solution)/shard_map/all_to_all | solution.py:40
  303.5 6.2 %all_to_all.57 = bf16[2,16,64,384]{3,2,1,0:T(8,128)(2,1)S(1)} all-to-all(bf16[2,16,64,384]{3,2,1,0:T(8,128)(2,1)S(1)} %broadcast_in_dim.48), channel_id=1, replica_groups=mesh['dp_0'=4,'dp_1'=4,'dp_2'=2,'mp_0'=4,'mp_1'=4] {'dp_2'}, dimensions={0} | all-to-all | bytes 3145728 | tf_op jit(solution)/shard_map/all_to_all | solution.py:40
  311.3 5.8 %all-gather.7 = f32[4,2,64]{2,1,0:T(2,128)S(1)} all-gather(f32[1,2,64]{2,1,0:T(2,128)S(1)} %maximum_bitcast_fusion), channel_id=4, replica_groups=mesh['dp_0'=4,'dp_1'=4,'dp_2'=2,'mp_0'=4,'mp_1'=4] {'dp_0'}, dimensions={0}, use_global_device_ids=true | all-gather | bytes 2560 | tf_op jit(solution)/shard_map/all_gather | solution.py:85
  317.2 6.7 %all-gather.8 = f32[4,2,64]{2,1,0:T(2,128)S(1)} all-gather(f32[1,2,64]{2,1,0:T(2,128)S(1)} %maximum_bitcast_fusion.1), channel_id=5, replica_groups=mesh['dp_0'=4,'dp_1'=4,'dp_2'=2,'mp_0'=4,'mp_1'=4] {'dp_1'}, dimensions={0}, use_global_device_ids=true | all-gather | bytes 2560 | tf_op jit(solution)/shard_map/all_gather | solution.py:85
  323.9 5.9 %all-gather.9 = f32[2,2,64]{2,1,0:T(2,128)S(1)} all-gather(f32[1,2,64]{2,1,0:T(2,128)S(1)} %maximum_bitcast_fusion.2), channel_id=6, replica_groups=mesh['dp_0'=4,'dp_1'=4,'dp_2'=2,'mp_0'=4,'mp_1'=4] {'dp_2'}, dimensions={0}, use_global_device_ids=true | all-gather | bytes 1536 | tf_op jit(solution)/shard_map/all_gather | solution.py:85
  329.8 7.2 %all-gather.10 = f32[4,2,64]{2,1,0:T(2,128)S(1)} all-gather(f32[1,2,64]{2,1,0:T(2,128)S(1)} %maximum_bitcast_fusion.3), channel_id=7, replica_groups=mesh['dp_0'=4,'dp_1'=4,'dp_2'=2,'mp_0'=4,'mp_1'=4] {'mp_0'}, dimensions={0}, use_global_device_ids=true | all-gather | bytes 2560 | tf_op jit(solution)/shard_map/all_gather | solution.py:85
  337.0 11.4 %all-gather.11 = f32[4,2,64]{2,1,0:T(2,128)S(1)} all-gather(f32[1,2,64]{2,1,0:T(2,128)S(1)} %maximum_bitcast_fusion.4), channel_id=8, replica_groups=mesh['dp_0'=4,'dp_1'=4,'dp_2'=2,'mp_0'=4,'mp_1'=4] {'mp_1'}, dimensions={0}, use_global_device_ids=true | all-gather | bytes 2560 | tf_op jit(solution)/shard_map/all_gather | solution.py:85
  (66 shorter events, 16.7 us)
Async XLA Ops:
  6.5 1.7 copy-start
  6.5 159.7 %all-gather.15.cloned.1.call-start = ((), (), s32[]{:S(2)}) async-start(), calls=%async_computation.8 | async-start | bytes 9732096 | tf_op jit(solution)/shard_map/all_gather | solution.py:145
  125.8 26.6 %all-to-all-start.2 = ((f32[32,1,128]{2,1,0:T(1,128)}), f32[32,1,128]{2,1,0:T(1,128)S(1)}, u32[]{:S(2)}, u32[]{:S(2)}) async-start(f32[32,1,128]{2,1,0:T(1,128)} %broadcast_in_dim.23), calls=%async_computation.2 | async-start | bytes 32768 | tf_op jit(solution)/shard_map/all_to_all | solution.py:40
  145.2 13.4 %copy-start.2 = (s32[2]{0:T(128)S(1)}, s32[2]{0:T(128)}, u32[]{:S(2)}) copy-start(s32[2]{0:T(128)} %param.10) | copy-start | bytes 28
  153.5 12.8 %all-to-all-start.3 = ((bf16[32,2,384]{2,1,0:T(2,128)(2,1)}), bf16[32,2,384]{2,1,0:T(2,128)(2,1)S(1)}, u32[]{:S(2)}, u32[]{:S(2)}) async-start(bf16[32,2,384]{2,1,0:T(2,128)(2,1)} %multiply_convert_fusion.1), calls=%async_computation.3 | async-start | bytes 98304 | tf_op jit(solution)/shard_map/all_to_all | solution.py:142
  158.6 103.5 %all-gather.17.cloned.1.call-start = ((), (), s32[]{:S(2)}) async-start(), calls=%async_computation.9 | async-start | bytes 1671168 | tf_op jit(solution)/shard_map/all_gather | solution.py:67
  171.3 14.2 %copy-start.1 = (bf16[384,384]{1,0:T(8,128)(2,1)S(1)}, bf16[384,384]{1,0:T(8,128)(2,1)}, u32[]{:S(2)}) copy-start(bf16[384,384]{1,0:T(8,128)(2,1)} %param.16) | copy-start | bytes 884740
  264.4 14.4 %all-to-all-start.5 = ((f32[32,1,128]{2,1,0:T(1,128)}), f32[32,1,128]{2,1,0:T(1,128)S(1)}, u32[]{:S(2)}, u32[]{:S(2)}) async-start(f32[32,1,128]{2,1,0:T(1,128)} %broadcast_in_dim.26), calls=%async_computation.5 | async-start | bytes 32768 | tf_op jit(solution)/shard_map/all_to_all | solution.py:40
Sparse Core Ops, SparseCore 0:
  9.5 120.3 all-gather.14
  186.4 75.6 all-gather.16
where the time goes:
time: 359 us; the launch traced here: 356 us
  blocking collectives  183 us (51%)
  waiting for transfers between devices  93 us (26%)
  starting transfers between devices  31.9 us (9%)
  local copies, waits for them, and re-layouts  16.1 us (4%)
  between operations  13.7 us (4%)
  matrix products  9.79 us (3%)
  other arithmetic  8.12 us (2%)
    all_gather x1, waiting for transfers between devices, over_pieces(): tiles = lax.all_gather(x, axis)  75.8 us
    all_gather x1, blocking collectives, total_of_pieces(): tiles = lax.all_gather(x, axis).astype(jnp.float32)  64.6 us
    all_to_all x3, blocking collectives, from_everyone(): return lax.all_to_all(copies, axis, split_axis=0, concat_axis=0, tiled=True)  41.2 us
    all_gather x5, blocking collectives, all_in_one(): both, at, found = (lax.all_gather(jnp.concatenate(lines), axis), 0, {})  36.9 us
    all_to_all x1, blocking collectives, sum_by_axis(): lax.all_to_all(own.astype(jnp.bfloat16), far, 0, 0, tiled=True)  28.3 us
    all_to_all x2, starting transfers between devices, from_everyone(): return lax.all_to_all(copies, axis, split_axis=0, concat_axis=0, tiled=True)  26.8 us
    all_to_all x1, blocking collectives, sent_and_summed(): tiles = lax.all_to_all(split_up(x, dim, devices), axis, 0, 0, tiled=True)  12.3 us
    all_to_all x2, waiting for transfers between devices, from_everyone(): return lax.all_to_all(copies, axis, split_axis=0, concat_axis=0, tiled=True)  8.92 us
  transfers between devices with their start and end apart: 5, of which 4 were waited for; matrix products, arithmetic and copies ran while one was open for 5% of the time, Pallas kernels for 0%

commit v1 on v0

v1 whole, which is shorter than its diff:
```python
import functools

import jax
import jax.numpy as jnp
from jax import lax
from jax.experimental import pallas as pl
from jax.experimental.pallas import tpu as pltpu
from jax.sharding import Mesh
from jax.sharding import PartitionSpec as P

HD = 128
EPS = 1e-5
DP_MP = ("dp_0", "dp_1", "dp_2", "mp_0", "mp_1")
DP = ("dp_0", "dp_1", "dp_2")
MP = ("mp_0", "mp_1")
MESH = pl.DeviceIdType.MESH
F32 = jnp.float32
BF16 = jnp.bfloat16
NSEM = 20


def kernel(
    sizes,
    ids_ref, len_ref, emb_ref, lng_ref, wq_ref, key_ref, val_ref, wo_ref, fg_ref,
    out_ref,
    emb, wq, key, val, wo,
    p, r1, r2, a3, r3, r4, r5, s1, s2, s3, s4,
    part, rq, ra, att_all, op, ro1, ro2, rs, fb, g1, g2, g3,
    load_sem, send_sem, recv_sem,
):
    Y, Z, C, X, H = sizes
    NDP, XY, ZC = Y * Z * C, X * Y, Z * C
    V, D = emb.shape
    SP, T, HW = key.shape
    W = D // NDP
    SEQ = SP * NDP
    R = SEQ // X
    NH = HW // HD

    yi, zi, ci, xi, hi = (lax.axis_index(a) for a in DP_MP)
    xy = xi * Y + yi
    zc = zi * C + ci
    dp = (yi * Z + zi) * C + ci

    def xy_dev(i):
        return {"mp_0": lax.div(i, Y), "dp_0": lax.rem(i, Y)}

    def zc_dev(i):
        return {"dp_1": lax.div(i, C), "dp_2": lax.rem(i, C)}

    def dp_dev(i):
        return {"dp_0": lax.div(i, ZC), "dp_1": lax.rem(lax.div(i, C), Z), "dp_2": lax.rem(i, C)}

    def z_dev(i):
        return {"dp_1": i}

    def c_dev(i):
        return {"dp_2": i}

    def x_dev(i):
        return {"mp_0": i}

    def h_dev(i):
        return {"mp_1": i}

    def each(n, body):
        if n <= 4:
            for k in range(1, n):
                body(k)
        else:
            lax.fori_loop(1, n, lambda k, _: body(k), None)

    def send(s, src, dst, dev):
        pltpu.make_async_remote_copy(
            src_ref=src, dst_ref=dst, send_sem=send_sem.at[s], recv_sem=recv_sem.at[s],
            device_id=dev, device_id_type=MESH,
        ).start()

    def take(sem, ref):
        pltpu.make_async_copy(ref, ref, sem).wait()

    pending = []

    def arrived(s, ref):
        take(recv_sem.at[s], ref)
        pending.append((s, ref))

    def exchange(s, src, dst, own, n, dev):
        def body(k):
            i = lax.rem(own + k, n)
            send(s, src.at[i], dst.at[own], dev(i))

        each(n, body)

    def gather(s, buf, own, n, dev):
        def body(k):
            i = lax.rem(own + k, n)
            send(s, buf.at[own], buf.at[own], dev(i))

        each(n, body)

    def to_rows(cols):
        n = cols[0].shape[0]
        lane = lax.broadcasted_iota(jnp.int32, (n, 128), 1)
        x = jnp.zeros((n, 128), F32)
        for k, col in enumerate(cols):
            x = jnp.where(lane == k, col, x)
        if n < 128:
            x = jnp.concatenate([x, jnp.zeros((128 - n, 128), F32)], axis=0)
        return jnp.transpose(x)

    def to_cols(rows):
        row = lax.broadcasted_iota(jnp.int32, (128, 128), 0)
        x = jnp.zeros((128, 128), F32)
        for k, r in enumerate(rows):
            x = jnp.where(row == k, r, x)
        return jnp.transpose(x)

    loads = [
        pltpu.make_async_copy(a, b, load_sem.at[i])
        for i, (a, b) in enumerate(
            ((emb_ref, emb), (wq_ref, wq), (key_ref, key), (val_ref, val), (wo_ref, wo))
        )
    ]
    for c in loads:
        c.start()

    barrier = pltpu.get_barrier_semaphore()

    def greet(dev):
        pl.semaphore_signal(barrier, inc=1, device_id=dev, device_id_type=MESH)

    each(H, lambda k: greet(h_dev(lax.rem(hi + k, H))))
    each(NDP, lambda k: greet(dp_dev(lax.rem(dp + k, NDP))))
    for kx in range(1, X):
        for ky in range(Y):
            greet({"mp_0": lax.rem(xi + kx, X), "dp_0": lax.rem(yi + ky, Y)})

    flat = (dp * X + xi) * H + hi
    ids = ids_ref[...]
    if SEQ < 128:
        ids = jnp.concatenate([ids, jnp.full((1, 128 - SEQ), -1, jnp.int32)], axis=1)
    row = lax.broadcasted_iota(jnp.int32, (128, 128), 0)
    hot = jnp.where((row + flat * V == ids) & (row < V), 1.0, 0.0).astype(F32)
    hot = jnp.transpose(hot)[:SEQ, :V].astype(BF16)

    loads[0].wait()
    other = 1 - ci
    acc = jnp.zeros((SEQ, 128), F32)
    for half in (other, ci):
        for yy in range(Y):
            for zz in range(Z):
                b = (yy * Z + zz) * C + half
                cols = pl.ds(pl.multiple_of(b * W, 128), W)
                blk = jnp.dot(hot, emb[:, cols], preferred_element_type=F32)
                for j in range(0, W, 128):
                    acc = acc + blk[:, j : j + 128]
                blk = blk.astype(BF16)
                for xx in range(X):
                    p[half, xx * Y + yy, zz] = blk[xx * R : (xx + 1) * R]
        if half is other:
            pl.semaphore_wait(barrier, NDP - 1 + (X - 1) * Y + H - 1)
            send(0, p.at[other], r1, c_dev(other))
    mean = jnp.sum(acc, axis=1, keepdims=True) / D
    devs = []
    for xx in range(X):
        m = mean[xx * R : (xx + 1) * R]
        sq = jnp.zeros((R, 128), F32)
        for cc in range(C):
            for yy in range(Y):
                for zz in range(Z):
                    d = p[cc, xx * Y + yy, zz].astype(F32) - m
                    for j in range(0, W, 128):
                        sq = sq + d[:, j : j + 128] * d[:, j : j + 128]
        devs.append(jnp.sum(sq, axis=1, keepdims=True) / D)
    var = jnp.concatenate(devs, axis=0)
    s1[ci] = to_rows((mean, var))[:8]
    gather(1, s1, ci, C, c_dev)

    arrived(0, r1)
    for k in range(XY):
        r1[k] = r1[k] + p[ci, k]
    exchange(2, r1, r2, xy, XY, xy_dev)
    r2[xy] = r1[xy]
    arrived(1, s1.at[pl.ds(0, C - 1)])
    s2[xy] = jnp.sum(s1[...], axis=0)
    gather(3, s2, xy, XY, xy_dev)

    arrived(2, r2.at[pl.ds(0, XY - 1)])
    for zz in range(Z):
        tot = r2[0, zz]
        for k in range(1, XY):
            tot = tot + r2[k, zz]
        a3[zz] = tot
    exchange(4, a3, r3, zi, Z, z_dev)
    r3[zi] = a3[zi]
    arrived(3, s2.at[pl.ds(0, XY - 1)])
    s3[zi] = jnp.sum(s2[...], axis=0)
    gather(5, s3, zi, Z, z_dev)

    arrived(4, r3.at[pl.ds(0, Z - 1)])
    tot = r3[0]
    for k in range(1, Z):
        tot = tot + r3[k]
    r4[hi] = tot
    if H > 1:
        gather(6, r4, hi, H, h_dev)
    arrived(5, s3.at[pl.ds(0, Z - 1)])
    s4[hi] = jnp.sum(s3[...], axis=0)
    if H > 1:
        gather(7, s4, hi, H, h_dev)

        arrived(6, r4.at[pl.ds(0, H - 1)])
    tot = r4[0]
    for k in range(1, H):
        tot = tot + r4[k]
    r5[xi] = tot
    gather(8, r5, xi, X, x_dev)
    if H > 1:
        arrived(7, s4.at[pl.ds(0, H - 1)])
    stats = jnp.sum(s4[...], axis=0)
    stats = to_cols((stats[0:1], stats[1:2]))
    mean, var = stats[:SEQ, 0:1], stats[:SEQ, 1:2]
    arrived(8, r5.at[pl.ds(0, X - 1)])

    own_cols = pl.ds(pl.multiple_of(dp * W, 128), W)
    embedded = r5[...].reshape(SEQ, W).astype(F32)
    normed = (lng_ref[:, own_cols] * (embedded - mean) * lax.rsqrt(var + EPS)).astype(BF16)
    loads[1].wait()
    partial = jnp.dot(normed, wq[...], preferred_element_type=F32)
    for j in range(NDP):
        part[j] = partial[j * SP : (j + 1) * SP]
    exchange(9, part, rq, dp, NDP, dp_dev)
    rq[dp] = part[dp]
    loads[2].wait()
    loads[3].wait()
    arrived(9, rq.at[pl.ds(0, NDP - 1)])
    queries = (jnp.sum(rq[...], axis=0) * HD**-0.5).astype(BF16).astype(F32)

    head = lax.broadcasted_iota(jnp.int32, (8, HW), 0) * HD
    lane = lax.broadcasted_iota(jnp.int32, (8, HW), 1)
    own_head = (lane >= head) & (lane < head + HD)
    place = lax.broadcasted_iota(jnp.int32, (8, T), 1)
    pair = lax.broadcasted_iota(jnp.int32, (SP, HW), 0)
    attended = jnp.zeros((SP, HW), F32)
    for s in range(SP):
        q = jnp.where(own_head, queries[s : s + 1], 0.0).astype(BF16)
        scores = lax.dot_general(
            q, key[s], (((1,), (1,)), ((), ())), preferred_element_type=F32
        )
        scores = jnp.where(place < len_ref[s], scores, -1e30)
        e = jnp.exp(scores - jnp.max(scores, axis=1, keepdims=True))
        w = (e / jnp.sum(e, axis=1, keepdims=True)).astype(BF16)
        got = jnp.dot(w, val[s], preferred_element_type=F32)
        got = jnp.sum(jnp.where(own_head, got, 0.0), axis=0, keepdims=True)
        attended = jnp.where(pair == s, got, attended)
    ra[dp] = attended.astype(BF16).astype(F32)
    gather(10, ra, dp, NDP, dp_dev)
    loads[4].wait()
    arrived(10, ra.at[pl.ds(0, NDP - 1)])
    for j in range(NDP):
        att_all[j * SP : (j + 1) * SP] = ra[j]

    mixed = jnp.dot(att_all[...].astype(BF16), wo[...], preferred_element_type=F32)
    for xx in range(X):
        op[xx] = mixed[xx * R : (xx + 1) * R]
    exchange(11, op, ro1, xi, X, x_dev)
    ro1[xi] = op[xi]
    arrived(11, ro1.at[pl.ds(0, X - 1)])
    ro2[hi] = jnp.sum(ro1[...], axis=0)
    if H > 1:
        gather(12, ro2, hi, H, h_dev)
        arrived(12, ro2.at[pl.ds(0, H - 1)])
    hidden = r5[xi].astype(F32) + jnp.sum(ro2[...], axis=0)

    m = jnp.sum(hidden, axis=1, keepdims=True) / W
    d = hidden - m
    rs[dp] = to_rows((m, jnp.sum(d * d, axis=1, keepdims=True)))[:2]
    gather(13, rs, dp, NDP, dp_dev)
    arrived(13, rs.at[pl.ds(0, NDP - 1)])
    blocks = rs[...]
    row_mean = jnp.sum(blocks, axis=0)[0:1] / NDP
    off = blocks[:, 0:1] - row_mean[None]
    row_var = jnp.sum(blocks[:, 1:2] + W * (off * off), axis=0) / D
    stats = to_cols((row_mean, lax.rsqrt(row_var + EPS)))
    fn = fg_ref[:, own_cols] * (hidden - stats[:R, 0:1]) * stats[:R, 1:2]
    fb[ci, xy, zi] = fn.astype(BF16)

    def f1(k):
        z = lax.rem(zi + k, Z)
        send(14, fb.at[ci, xy, zi], fb.at[ci, xy, zi], z_dev(z))

    each(Z, f1)
    arrived(14, fb.at[ci, xy, pl.ds(0, Z - 1)])

    def f2(k):
        i = lax.rem(xy + k, XY)
        send(15, fb.at[ci, xy], fb.at[ci, xy], xy_dev(i))

    each(XY, f2)
    arrived(15, fb.at[ci, pl.ds(0, XY - 1)])
    send(16, fb.at[ci], fb.at[ci], c_dev(other))
    arrived(16, fb.at[other])

    logits = jnp.zeros((SEQ, V), F32)
    for yy in range(Y):
        for zz in range(Z):
            lhs = jnp.concatenate(
                [
                    jnp.concatenate([fb[cc, xx * Y + yy, zz] for xx in range(X)], axis=0)
                    for cc in range(C)
                ],
                axis=1,
            )
            b = (yy * Z + zz) * C * W
            logits = logits + lax.dot_general(
                lhs, emb[:, b : b + C * W], (((1,), (1,)), ((), ())), preferred_element_type=F32
            )
    top = jnp.max(logits, axis=1, keepdims=True)
    total = jnp.sum(jnp.exp(logits - top), axis=1, keepdims=True)
    slab = to_rows((top, total))[:2]

    def merged(buf):
        v = buf[...]
        tops, sums = v[:, 0:1], v[:, 1:2]
        best = jnp.max(tops, axis=0)
        return best, jnp.sum(sums * jnp.exp(tops - best[None]), axis=0)

    def joined(best, tot):
        r = lax.broadcasted_iota(jnp.int32, (2, 128), 0)
        return jnp.where(r == 0, best, tot)

    g1[xy] = slab
    gather(17, g1, xy, XY, xy_dev)
    arrived(17, g1.at[pl.ds(0, XY - 1)])
    g2[zc] = joined(*merged(g1))
    gather(18, g2, zc, ZC, zc_dev)
    arrived(18, g2.at[pl.ds(0, ZC - 1)])
    g3[hi] = joined(*merged(g2))
    if H > 1:
        gather(19, g3, hi, H, h_dev)
        arrived(19, g3.at[pl.ds(0, H - 1)])
    best, tot = merged(g3)
    stats = to_cols((best, jnp.log(tot)))
    out_ref[...] = (logits - stats[:SEQ, 0:1]) - stats[:SEQ, 1:2]
    for s, ref in pending:
        take(send_sem.at[s], ref)


def per_device(sizes, token_ids, cache_lengths, embedding, ln_gain, query_weight, key_cache,
               value_cache, out_weight, final_gain):
    Y, Z, C, X, H = sizes
    NDP, XY = Y * Z * C, X * Y
    V, D = embedding.shape
    SP, T, HW = key_cache.shape
    W = D // NDP
    SEQ = SP * NDP
    R = SEQ // X
    vmem = pl.BlockSpec(memory_space=pltpu.VMEM)
    smem = pl.BlockSpec(memory_space=pltpu.SMEM)
    hbm = pl.BlockSpec(memory_space=pl.ANY)
    return pl.pallas_call(
        functools.partial(kernel, sizes),
        name="decode",
        out_shape=jax.ShapeDtypeStruct((SEQ, V), F32),
        in_specs=[vmem, smem, hbm, vmem, hbm, hbm, hbm, hbm, vmem],
        out_specs=vmem,
        scratch_shapes=[
            pltpu.VMEM((V, D), BF16),
            pltpu.VMEM((W, HW), BF16),
            pltpu.VMEM((SP, T, HW), BF16),
            pltpu.VMEM((SP, T, HW), BF16),
            pltpu.VMEM((HW, W), BF16),
            pltpu.VMEM((C, XY, Z, R, W), BF16),
            pltpu.VMEM((XY, Z, R, W), BF16),
            pltpu.VMEM((XY, Z, R, W), BF16),
            pltpu.VMEM((Z, R, W), BF16),
            pltpu.VMEM((Z, R, W), BF16),
            pltpu.VMEM((H, R, W), BF16),
            pltpu.VMEM((X, R, W), BF16),
            pltpu.VMEM((C, 8, 128), F32),
            pltpu.VMEM((XY, 8, 128), F32),
            pltpu.VMEM((Z, 8, 128), F32),
            pltpu.VMEM((H, 8, 128), F32),
            pltpu.VMEM((NDP, SP, HW), F32),
            pltpu.VMEM((NDP, SP, HW), F32),
            pltpu.VMEM((NDP, SP, HW), F32),
            pltpu.VMEM((SEQ, HW), F32),
            pltpu.VMEM((X, R, W), F32),
            pltpu.VMEM((X, R, W), F32),
            pltpu.VMEM((H, R, W), F32),
            pltpu.VMEM((NDP, 2, 128), F32),
            pltpu.VMEM((C, XY, Z, R, W), BF16),
            pltpu.VMEM((XY, 2, 128), F32),
            pltpu.VMEM((Z * C, 2, 128), F32),
            pltpu.VMEM((H, 2, 128), F32),
            pltpu.SemaphoreType.DMA((5,)),
            pltpu.SemaphoreType.DMA((NSEM,)),
            pltpu.SemaphoreType.DMA((NSEM,)),
        ],
        compiler_params=pltpu.CompilerParams(collective_id=0, has_side_effects=True),
    )(
        token_ids.reshape(1, -1), cache_lengths, embedding, ln_gain.reshape(1, -1), query_weight,
        key_cache, value_cache, out_weight, final_gain.reshape(1, -1),
    )


def solution(mesh, sizes=(4, 4, 2, 4, 4)):
    finer = Mesh(mesh.devices.reshape(sizes), DP_MP)
    placed = (
        P(),
        P(DP),
        P(DP_MP, None),
        P(),
        P(DP, MP),
        P(DP, None, MP),
        P(DP, None, MP),
        P(MP, DP),
        P(),
    )
    return jax.shard_map(
        functools.partial(per_device, sizes), mesh=finer, in_specs=placed,
        out_specs=P(None, DP_MP), check_vma=False,
    )
```

time: 359 us -> 115 us (0.32)
  blocking collectives: 183 us -> 0 us
  Pallas kernels: 0 us -> 113 us
  waiting for transfers between devices: 93 us -> 0 us
  starting transfers between devices: 31.9 us -> 0 us
  local copies, waits for them, and re-layouts: 16.1 us -> 1.38 us
  between operations: 13.7 us -> 0.01 us
  matrix products: 9.79 us -> 0 us
  other arithmetic: 8.12 us -> 0 us
    pallas_call x0 -> x1, Pallas kernels: none -> 113 us  [per_device(): pl.pallas_call(functools.partial(kernel, sizes), name='decode', out_shape...]
    all_gather x6 -> x0, blocking collectives: 102 us -> none  [the longest x1 64.6 us: total_of_pieces(): tiles = lax.all_gather(x, axis).astype(jnp.float32)]
    all_to_all x5 -> x0, blocking collectives: 81.8 us -> none  [the longest x3 41.2 us: from_everyone(): return lax.all_to_all(copies, axis, split_axis=0, concat_axis=0, tiled=True)]
    all_gather x2 -> x0, waiting for transfers between devices: 75.8 us -> none  [the longest x1 75.8 us: over_pieces(): tiles = lax.all_gather(x, axis)]
    all_to_all x3 -> x0, starting transfers between devices: 31.9 us -> none  [the longest x2 26.8 us: from_everyone(): return lax.all_to_all(copies, axis, split_axis=0, concat_axis=0, tiled=True)]
    all_to_all x3 -> x0, waiting for transfers between devices: 16.4 us -> none  [the longest x2 8.92 us: from_everyone(): return lax.all_to_all(copies, axis, split_axis=0, concat_axis=0, tiled=True)]
    dot_general x6 -> x0, matrix products: 9.79 us -> none  [the longest x1 5 us: per_device(): jnp.dot(own_rows, lax.all_gather(query_weight, DP, axis=0, tiled=True), p...]
    reshape x5 -> x0, local copies, waits for them, and re-layouts: 5.94 us -> none  [the longest x2 5.72 us: split_up(): x.reshape(*shape[:dim], devices, shape[dim] // devices, *shape[dim + 1:])]
  transfers between devices with their start and end apart: 5 -> 0, of which waited for: 4 -> 0; matrix products, arithmetic and copies ran while one was open for 5% -> 0% of each run, Pallas kernels for 0% -> 0%
where the time goes in v1:
time: 115 us
  Pallas kernels  113 us (98%)
  local copies, waits for them, and re-layouts  1.38 us (1%)
    pallas_call x1, Pallas kernels, per_device(): pl.pallas_call(functools.partial(kernel, sizes), name='decode', out_shape...  113 us

profile of v1, /device:TPU:1, one launch (start us, length us, event | category | flops | bytes accessed | tf_op | source)
XLA Modules:
  0.0 114.6 jit_solution(11758488644417197171)
XLA Ops:
  0.0 113.2 %decode.1 = f32[64,96]{1,0:T(8,128)} custom-call(s32[1,64]{1,0:T(1,128)} %bitcast.5, s32[2]{0:T(128)} %len_ref.1, bf16[96,12288]{1,0:T(8,128)(2,1)} %emb_ref.1, f32[1,12288]{1,0:T(1,128)} %bitcast.3, bf16[384,384]{1,0:T(8,128)(2,1)} %wq_ref.1, bf16[2,512,384]{2,1,0:T(8,128)(2,1)} %key_ref.1, bf16[2,512,384]{2,1,0:T(8,128)(2,1)} %val_ref.1, ...), custom_call_target="tpu_custom_call" | custom-call | tf_op jit(solution)/shard_map/decode/pallas_call | solution.py:362
  113.2 1.4 %copy.11 = f32[64,96]{1,0:T(8,128)} copy(f32[64,96]{1,0:T(8,128)} %decode.1) | data formatting | bytes 49152

commit v2 on v1

v2 whole, which is shorter than its diff:
```python
import functools

import jax
import jax.numpy as jnp
from jax import lax
from jax.experimental import pallas as pl
from jax.experimental.pallas import tpu as pltpu
from jax.sharding import Mesh
from jax.sharding import PartitionSpec as P

HD = 128
EPS = 1e-5
DP_MP = ("dp_0", "dp_1", "dp_2", "mp_0", "mp_1")
DP = ("dp_0", "dp_1", "dp_2")
MP = ("mp_0", "mp_1")
MESH = pl.DeviceIdType.MESH
F32 = jnp.float32
BF16 = jnp.bfloat16
NSEM = 36


def kernel(
    sizes,
    ids_ref, len_ref, emb_ref, lng_ref, wq_ref, key_ref, val_ref, wo_ref, fg_ref,
    out_ref,
    emb, wq, key, val, wo,
    p, r1, a1, a2, a3, b1, b2, b3, t0, r3, r4, r5, s1, s2, s3, s4,
    part, rq, ra, att_all, op, ro1, ro2, gmat, dm, fb, fs, g1, g2,
    load_sem, send_sem, recv_sem,
):
    Y, Z, C, X, H = sizes
    NDP, XY, ZC, ZH = Y * Z * C, X * Y, Z * C, Z // 2
    V, D = emb.shape
    SP, T, HW = key.shape
    W = D // NDP
    SEQ = SP * NDP
    R = SEQ // X
    NH = HW // HD

    yi, zi, ci, xi, hi = (lax.axis_index(a) for a in DP_MP)
    xy = xi * Y + yi
    zz_own = hi * Z + zi
    xyc = xy * C + ci
    dp = (yi * Z + zi) * C + ci

    def xy_dev(i):
        return {"mp_0": lax.div(i, Y), "dp_0": lax.rem(i, Y)}

    def xyc_dev(i):
        return {"dp_2": lax.rem(i, C), **xy_dev(lax.div(i, C))}

    def zz_dev(i):
        return {"mp_1": lax.div(i, Z), "dp_1": lax.rem(i, Z)}

    def dp_dev(i):
        return {"dp_0": lax.div(i, ZC), "dp_1": lax.rem(lax.div(i, C), Z), "dp_2": lax.rem(i, C)}

    def y_dev(i):
        return {"dp_0": i}

    def z_dev(i):
        return {"dp_1": i}

    def c_dev(i):
        return {"dp_2": i}

    def x_dev(i):
        return {"mp_0": i}

    def h_dev(i):
        return {"mp_1": i}

    def each(n, body):
        if n <= 4:
            for k in range(1, n):
                body(k)
        else:
            lax.fori_loop(1, n, lambda k, _: body(k), None)

    def send(s, src, dst, dev):
        pltpu.make_async_remote_copy(
            src_ref=src, dst_ref=dst, send_sem=send_sem.at[s], recv_sem=recv_sem.at[s],
            device_id=dev, device_id_type=MESH,
        ).start()

    def take(sem, ref):
        pltpu.make_async_copy(ref, ref, sem).wait()

    pending = []
    used = [0]

    def new():
        used[0] += 1
        return used[0] - 1

    def arrived(s, ref):
        take(recv_sem.at[s], ref)
        pending.append((s, ref))

    def exchange(src, dst, own, n, dev):
        s = new()

        def body(k):
            i = lax.rem(own + k, n)
            send(s, src(i), dst, dev(i))

        each(n, body)
        return s

    def gather(buf, own, n, dev):
        return exchange(lambda i: buf.at[own], buf.at[own], own, n, dev)

    def to_rows(cols, start=None):
        n = cols[0].shape[0]
        lane = lax.broadcasted_iota(jnp.int32, (n, 128), 1)
        x = jnp.zeros((n, 128), F32)
        for k, col in enumerate(cols):
            x = jnp.where(lane == k, col, x)
        if start is not None:
            x = jnp.concatenate([x] * (SEQ // n), axis=0)
            r = lax.broadcasted_iota(jnp.int32, (SEQ, 128), 0)
            x = jnp.where((r >= start) & (r < start + n), x, 0.0)
        if x.shape[0] < 128:
            x = jnp.concatenate([x, jnp.zeros((128 - x.shape[0], 128), F32)], axis=0)
        return jnp.transpose(x)

    def to_cols(rows):
        row = lax.broadcasted_iota(jnp.int32, (128, 128), 0)
        x = jnp.zeros((128, 128), F32)
        for k, r in enumerate(rows):
            x = jnp.where(row == k, r, x)
        return jnp.transpose(x)

    loads = [
        pltpu.make_async_copy(a, b, load_sem.at[i])
        for i, (a, b) in enumerate(
            ((emb_ref, emb), (wq_ref, wq), (key_ref, key), (val_ref, val), (wo_ref, wo))
        )
    ]
    for c in loads:
        c.start()

    barrier = pltpu.get_barrier_semaphore()

    def greet(dev):
        pl.semaphore_signal(barrier, inc=1, device_id=dev, device_id_type=MESH)

    for kh in range(1, H):
        for kz in range(Z):
            greet({"mp_1": lax.rem(hi + kh, H), "dp_1": lax.rem(zi + kz, Z)})
    each(NDP, lambda k: greet(dp_dev(lax.rem(dp + k, NDP))))
    for kx in range(1, X):
        for ky in range(Y):
            for kc in range(C):
                greet({
                    "mp_0": lax.rem(xi + kx, X),
                    "dp_0": lax.rem(yi + ky, Y),
                    "dp_2": lax.rem(ci + kc, C),
                })
    greeted = NDP - 1 + (X - 1) * Y * C + (H - 1) * Z

    flat = (dp * X + xi) * H + hi
    ids = ids_ref[...]
    if SEQ < 128:
        ids = jnp.concatenate([ids, jnp.full((1, 128 - SEQ), -1, jnp.int32)], axis=1)
    row = lax.broadcasted_iota(jnp.int32, (128, 128), 0)
    hot = jnp.where((row + flat * V == ids) & (row < V), 1.0, 0.0).astype(F32)
    hot = jnp.transpose(hot)[:SEQ, :V].astype(BF16)

    loads[0].wait()
    other = 1 - ci
    acc = jnp.zeros((SEQ, 128), F32)

    def rows_of(acc, core, half):
        for yy in range(Y):
            for zz in range(ZH):
                b = (yy * Z + half * ZH + zz) * C + core
                cols = pl.ds(pl.multiple_of(b * W, 128), W)
                blk = jnp.dot(hot, emb[:, cols], preferred_element_type=F32)
                for j in range(0, W, 128):
                    acc = acc + blk[:, j : j + 128]
                blk = blk.astype(BF16)
                for xx in range(X):
                    p[core, half, yy, xx, zz] = blk[xx * R : (xx + 1) * R]
        return acc

    def to_core(half):
        s = new()
        send(s, p.at[other, half], r1.at[half], c_dev(other))
        return s

    def summed(half):
        for yy in range(Y):
            for xx in range(X):
                r1[half, yy, xx] = r1[half, yy, xx] + p[ci, half, yy, xx]

    acc = rows_of(acc, other, 0)
    pl.semaphore_wait(barrier, greeted)
    e1a = to_core(0)
    acc = rows_of(acc, other, 1)
    e1b = to_core(1)
    acc = rows_of(acc, ci, 0)
    arrived(e1a, r1.at[0])
    summed(0)
    ea = exchange(lambda i: r1.at[0, :, i], a1.at[xi], xi, X, x_dev)
    acc = rows_of(acc, ci, 1)
    arrived(e1b, r1.at[1])
    summed(1)
    eb = exchange(lambda i: r1.at[1, i], b1.at[yi], yi, Y, y_dev)
    a1[xi] = r1[0, :, xi]
    b1[yi] = r1[1, yi]

    mean = jnp.sum(acc, axis=1, keepdims=True) / D
    devs = []
    for xx in range(X):
        m = mean[xx * R : (xx + 1) * R]
        sq = jnp.zeros((R, 128), F32)
        for cc in range(C):
            for hh in range(2):
                for yy in range(Y):
                    for zz in range(ZH):
                        d = p[cc, hh, yy, xx, zz].astype(F32) - m
                        for j in range(0, W, 128):
                            sq = sq + d[:, j : j + 128] * d[:, j : j + 128]
        devs.append(jnp.sum(sq, axis=1, keepdims=True) / D)
    var = jnp.concatenate(devs, axis=0)
    s1[ci] = to_rows((mean, var))[:8]
    es = gather(s1, ci, C, c_dev)

    arrived(ea, a1.at[pl.ds(0, X - 1)])
    for yy in range(Y):
        tot = a1[0, yy]
        for k in range(1, X):
            tot = tot + a1[k, yy]
        a2[yy] = tot
    ea = exchange(lambda i: a2.at[i], a3.at[yi], yi, Y, y_dev)
    a3[yi] = a2[yi]
    arrived(es, s1.at[pl.ds(0, C - 1)])
    s2[xy] = jnp.sum(s1[...], axis=0)
    es = gather(s2, xy, XY, xy_dev)
    arrived(eb, b1.at[pl.ds(0, Y - 1)])
    for xx in range(X):
        tot = b1[0, xx]
        for k in range(1, Y):
            tot = tot + b1[k, xx]
        b2[xx] = tot
    eb = exchange(lambda i: b2.at[i], b3.at[xi], xi, X, x_dev)
    b3[xi] = b2[xi]

    half_row = lax.broadcasted_iota(jnp.int32, (16, W), 0)
    for j in range(NDP):
        gain = fg_ref[:, j * W : (j + 1) * W]
        high = gain.astype(BF16).astype(F32)
        both = jnp.where(half_row == 0, high, jnp.where(half_row == 1, gain - high, 0.0))
        got = lax.dot_general(
            both.astype(BF16), emb[:, j * W : (j + 1) * W], (((1,), (1,)), ((), ())),
            preferred_element_type=F32,
        )
        gmat[j : j + 1] = got[0:1] + got[1:2]

    arrived(ea, a3.at[pl.ds(0, Y - 1)])
    tot = a3[0]
    for k in range(1, Y):
        tot = tot + a3[k]
    t0[0:ZH] = tot
    arrived(eb, b3.at[pl.ds(0, X - 1)])
    tot = b3[0]
    for k in range(1, X):
        tot = tot + b3[k]
    t0[ZH:Z] = tot
    ez = exchange(lambda i: t0.at[i], r3.at[zi], zi, Z, z_dev)
    r3[zi] = t0[zi]
    arrived(es, s2.at[pl.ds(0, XY - 1)])
    s3[zi] = jnp.sum(s2[...], axis=0)
    es = gather(s3, zi, Z, z_dev)

    arrived(ez, r3.at[pl.ds(0, Z - 1)])
    tot = r3[0]
    for k in range(1, Z):
        tot = tot + r3[k]
    r4[hi] = tot
    if H > 1:
        ez = gather(r4, hi, H, h_dev)
    arrived(es, s3.at[pl.ds(0, Z - 1)])
    s4[hi] = jnp.sum(s3[...], axis=0)
    if H > 1:
        es = gather(s4, hi, H, h_dev)
        arrived(ez, r4.at[pl.ds(0, H - 1)])
    tot = r4[0]
    for k in range(1, H):
        tot = tot + r4[k]
    r5[xi] = tot
    ex = gather(r5, xi, X, x_dev)
    if H > 1:
        arrived(es, s4.at[pl.ds(0, H - 1)])
    stats = jnp.sum(s4[...], axis=0)
    stats = to_cols((stats[0:1], stats[1:2]))
    mean, var = stats[:SEQ, 0:1], stats[:SEQ, 1:2]
    arrived(ex, r5.at[pl.ds(0, X - 1)])

    own_cols = pl.ds(pl.multiple_of(dp * W, 128), W)
    embedded = r5[...].reshape(SEQ, W).astype(F32)
    normed = (lng_ref[:, own_cols] * (embedded - mean) * lax.rsqrt(var + EPS)).astype(BF16)
    loads[1].wait()
    partial = jnp.dot(normed, wq[...], preferred_element_type=F32)
    for j in range(NDP):
        part[j] = partial[j * SP : (j + 1) * SP]
    eq = exchange(lambda i: part.at[i], rq.at[dp], dp, NDP, dp_dev)
    rq[dp] = part[dp]
    loads[2].wait()
    loads[3].wait()
    arrived(eq, rq.at[pl.ds(0, NDP - 1)])
    queries = (jnp.sum(rq[...], axis=0) * HD**-0.5).astype(BF16).astype(F32)

    head = lax.broadcasted_iota(jnp.int32, (8, HW), 0) * HD
    lane = lax.broadcasted_iota(jnp.int32, (8, HW), 1)
    own_head = (lane >= head) & (lane < head + HD)
    place = lax.broadcasted_iota(jnp.int32, (8, T), 1)
    pair = lax.broadcasted_iota(jnp.int32, (SP, HW), 0)
    attended = jnp.zeros((SP, HW), F32)
    for s in range(SP):
        q = jnp.where(own_head, queries[s : s + 1], 0.0).astype(BF16)
        scores = lax.dot_general(
            q, key[s], (((1,), (1,)), ((), ())), preferred_element_type=F32
        )
        scores = jnp.where(place < len_ref[s], scores, -1e30)
        e = jnp.exp(scores - jnp.max(scores, axis=1, keepdims=True))
        w = (e / jnp.sum(e, axis=1, keepdims=True)).astype(BF16)
        got = jnp.dot(w, val[s], preferred_element_type=F32)
        got = jnp.sum(jnp.where(own_head, got, 0.0), axis=0, keepdims=True)
        attended = jnp.where(pair == s, got, attended)
    ra[dp] = attended.astype(BF16).astype(F32)
    eg = gather(ra, dp, NDP, dp_dev)
    loads[4].wait()
    arrived(eg, ra.at[pl.ds(0, NDP - 1)])
    for j in range(NDP):
        att_all[j * SP : (j + 1) * SP] = ra[j]

    mixed = jnp.dot(att_all[...].astype(BF16), wo[...], preferred_element_type=F32)
    for xx in range(X):
        op[xx] = mixed[xx * R : (xx + 1) * R]
    eo = exchange(lambda i: op.at[i], ro1.at[xi], xi, X, x_dev)
    ro1[xi] = op[xi]
    arrived(eo, ro1.at[pl.ds(0, X - 1)])
    ro2[hi] = jnp.sum(ro1[...], axis=0).astype(BF16)
    if H > 1:
        eo = gather(ro2, hi, H, h_dev)
        arrived(eo, ro2.at[pl.ds(0, H - 1)])
    hidden = r5[xi].astype(F32) + jnp.sum(ro2[...].astype(F32), axis=0)

    m = jnp.sum(hidden, axis=1, keepdims=True) / W
    d = hidden - m
    zh, zl = lax.div(zi, ZH), lax.rem(zi, ZH)
    fb[zh, ci, xi, yi, zl] = (fg_ref[:, own_cols] * d).astype(BF16)
    ef = exchange(
        lambda i: fb.at[zh, ci, xi, yi, zl], fb.at[zh, ci, xi, yi, zl], zi, Z, z_dev
    )
    fs[ci, xy, zi] = to_rows((m, jnp.sum(d * d, axis=1, keepdims=True)), xi * R)[:2]
    es = exchange(lambda i: fs.at[ci, xy, zi], fs.at[ci, xy, zi], zi, Z, z_dev)

    arrived(ef, fb.at[0, 0, 0, pl.ds(0, Z - 1), 0])
    ea = exchange(lambda i: fb.at[0, ci, xi, yi], fb.at[0, ci, xi, yi], yi, Y, y_dev)
    eb = exchange(lambda i: fb.at[1, ci, xi, yi], fb.at[1, ci, xi, yi], xi, X, x_dev)
    arrived(es, fs.at[ci, xy, pl.ds(0, Z - 1)])
    es = exchange(lambda i: fs.at[ci, xy], fs.at[ci, xy], xy, XY, xy_dev)
    arrived(ea, fb.at[0, ci, xi, pl.ds(0, Y - 1)])
    ea = exchange(lambda i: fb.at[0, ci, xi], fb.at[0, ci, xi], xi, X, x_dev)
    arrived(eb, fb.at[1, ci, pl.ds(0, X - 1), yi])
    eb = exchange(lambda i: fb.at[1, ci, :, yi], fb.at[1, ci, :, yi], yi, Y, y_dev)
    arrived(es, fs.at[ci, pl.ds(0, XY - 1)])
    es = exchange(lambda i: fs.at[ci], fs.at[ci], ci, C, c_dev)

    def products(logits, core, half):
        for yy in range(Y):
            lhs = jnp.concatenate(
                [
                    jnp.concatenate([fb[half, core, xx, yy, zz] for xx in range(X)], axis=0)
                    for zz in range(ZH)
                ],
                axis=1,
            )
            rhs = jnp.concatenate(
                [
                    emb[:, pl.ds(pl.multiple_of(
                        ((yy * Z + half * ZH + zz) * C + core) * W, 128), W)]
                    for zz in range(ZH)
                ],
                axis=1,
            )
            logits = logits + lax.dot_general(
                lhs, rhs, (((1,), (1,)), ((), ())), preferred_element_type=F32
            )
        return logits

    logits = jnp.zeros((SEQ, V), F32)
    arrived(ea, fb.at[0, ci, pl.ds(0, X - 1)])
    ea = exchange(lambda i: fb.at[0, ci], fb.at[0, ci], ci, C, c_dev)
    arrived(eb, fb.at[1, ci, :, pl.ds(0, Y - 1)])
    eb = exchange(lambda i: fb.at[1, ci], fb.at[1, ci], ci, C, c_dev)
    arrived(es, fs.at[ci])
    row_mean = jnp.zeros((1, 128), F32)
    row_var = jnp.zeros((1, 128), F32)
    blocks = []
    for yy in range(Y):
        for zz in range(Z):
            for cc in range(C):
                b = fs[cc, yy, zz]
                for xx in range(1, X):
                    b = b + fs[cc, xx * Y + yy, zz]
                row_mean = row_mean + b[0:1]
                row_var = row_var + b[1:2]
                blocks.append(b[0:1])
    row_mean = row_mean / NDP
    for j in range(NDP):
        off = blocks[j] - row_mean
        row_var = row_var + W * (off * off)
        dm[j : j + 1] = off
    scale = to_cols((lax.rsqrt(row_var / D + EPS),))[:SEQ, 0:1]
    offs = jnp.transpose(dm[...])[:SEQ, :NDP]
    logits = logits + jnp.dot(
        offs, gmat[...], preferred_element_type=F32, precision=lax.Precision.HIGHEST
    )
    logits = products(logits, ci, 0)
    logits = products(logits, ci, 1)
    arrived(ea, fb.at[0, other])
    logits = products(logits, other, 0)
    arrived(eb, fb.at[1, other])
    logits = products(logits, other, 1) * scale

    top = jnp.max(logits, axis=1, keepdims=True)
    total = jnp.sum(jnp.exp(logits - top), axis=1, keepdims=True)

    def merged(buf):
        v = buf[...]
        tops, sums = v[:, 0:1], v[:, 1:2]
        best = jnp.max(tops, axis=0)
        return best, jnp.sum(sums * jnp.exp(tops - best[None]), axis=0)

    def joined(best, tot):
        r = lax.broadcasted_iota(jnp.int32, (2, 128), 0)
        return jnp.where(r == 0, best, tot)

    g1[xyc] = to_rows((top, total))[:2]
    eg = gather(g1, xyc, XY * C, xyc_dev)
    arrived(eg, g1.at[pl.ds(0, XY * C - 1)])
    g2[zz_own] = joined(*merged(g1))
    eg = gather(g2, zz_own, Z * H, zz_dev)
    arrived(eg, g2.at[pl.ds(0, Z * H - 1)])
    best, tot = merged(g2)
    stats = to_cols((best, jnp.log(tot)))
    out_ref[...] = (logits - stats[:SEQ, 0:1]) - stats[:SEQ, 1:2]
    for s, ref in pending:
        take(send_sem.at[s], ref)


def per_device(sizes, token_ids, cache_lengths, embedding, ln_gain, query_weight, key_cache,
               value_cache, out_weight, final_gain):
    Y, Z, C, X, H = sizes
    NDP, XY, ZH = Y * Z * C, X * Y, Z // 2
    V, D = embedding.shape
    SP, T, HW = key_cache.shape
    W = D // NDP
    SEQ = SP * NDP
    R = SEQ // X
    vmem = pl.BlockSpec(memory_space=pltpu.VMEM)
    smem = pl.BlockSpec(memory_space=pltpu.SMEM)
    hbm = pl.BlockSpec(memory_space=pl.ANY)
    return pl.pallas_call(
        functools.partial(kernel, sizes),
        name="decode",
        out_shape=jax.ShapeDtypeStruct((SEQ, V), F32),
        in_specs=[vmem, smem, hbm, vmem, hbm, hbm, hbm, hbm, vmem],
        out_specs=vmem,
        scratch_shapes=[
            pltpu.VMEM((V, D), BF16),
            pltpu.VMEM((W, HW), BF16),
            pltpu.VMEM((SP, T, HW), BF16),
            pltpu.VMEM((SP, T, HW), BF16),
            pltpu.VMEM((HW, W), BF16),
            pltpu.VMEM((C, 2, Y, X, ZH, R, W), BF16),
            pltpu.VMEM((2, Y, X, ZH, R, W), BF16),
            pltpu.VMEM((X, Y, ZH, R, W), BF16),
            pltpu.VMEM((Y, ZH, R, W), BF16),
            pltpu.VMEM((Y, ZH, R, W), BF16),
            pltpu.VMEM((Y, X, ZH, R, W), BF16),
            pltpu.VMEM((X, ZH, R, W), BF16),
            pltpu.VMEM((X, ZH, R, W), BF16),
            pltpu.VMEM((Z, R, W), BF16),
            pltpu.VMEM((Z, R, W), BF16),
            pltpu.VMEM((H, R, W), BF16),
            pltpu.VMEM((X, R, W), BF16),
            pltpu.VMEM((C, 8, 128), F32),
            pltpu.VMEM((XY, 8, 128), F32),
            pltpu.VMEM((Z, 8, 128), F32),
            pltpu.VMEM((H, 8, 128), F32),
            pltpu.VMEM((NDP, SP, HW), F32),
            pltpu.VMEM((NDP, SP, HW), F32),
            pltpu.VMEM((NDP, SP, HW), F32),
            pltpu.VMEM((SEQ, HW), F32),
            pltpu.VMEM((X, R, W), F32),
            pltpu.VMEM((X, R, W), F32),
            pltpu.VMEM((H, R, W), BF16),
            pltpu.VMEM((NDP, V), F32),
            pltpu.VMEM((max(NDP, 128), 128), F32),
            pltpu.VMEM((2, C, X, Y, ZH, R, W), BF16),
            pltpu.VMEM((C, XY, Z, 2, 128), F32),
            pltpu.VMEM((XY * C, 2, 128), F32),
            pltpu.VMEM((Z * H, 2, 128), F32),
            pltpu.SemaphoreType.DMA((5,)),
            pltpu.SemaphoreType.DMA((NSEM,)),
            pltpu.SemaphoreType.DMA((NSEM,)),
        ],
        compiler_params=pltpu.CompilerParams(collective_id=0, has_side_effects=True),
    )(
        token_ids.reshape(1, -1), cache_lengths, embedding, ln_gain.reshape(1, -1), query_weight,
        key_cache, value_cache, out_weight, final_gain.reshape(1, -1),
    )


def solution(mesh, sizes=(4, 4, 2, 4, 4)):
    finer = Mesh(mesh.devices.reshape(sizes), DP_MP)
    placed = (
        P(),
        P(DP),
        P(DP_MP, None),
        P(),
        P(DP, MP),
        P(DP, None, MP),
        P(DP, None, MP),
        P(MP, DP),
        P(),
    )
    return jax.shard_map(
        functools.partial(per_device, sizes), mesh=finer, in_specs=placed,
        out_specs=P(None, DP_MP), check_vma=False,
    )
```

time: 115 us -> 98.9 us (0.86)
  Pallas kernels: 113 us -> 97.3 us
    pallas_call x1, Pallas kernels: 113 us -> 97.3 us  [per_device(): pl.pallas_call(functools.partial(kernel, sizes), name='decode', out_shape...]
where the time goes in v2:
time: 98.9 us; the launch traced here: 98.7 us
  Pallas kernels  97.3 us (98%)
  local copies, waits for them, and re-layouts  1.38 us (1%)
    pallas_call x1, Pallas kernels, per_device(): pl.pallas_call(functools.partial(kernel, sizes), name='decode', out_shape...  97.3 us

profile of v2, /device:TPU:1, one launch (start us, length us, event | category | flops | bytes accessed | tf_op | source)
XLA Modules:
  0.0 98.7 jit_solution(11915618137393642867)
XLA Ops:
  0.0 97.3 %decode.1 = f32[64,96]{1,0:T(8,128)} custom-call(s32[1,64]{1,0:T(1,128)} %bitcast.5, s32[2]{0:T(128)} %len_ref.1, bf16[96,12288]{1,0:T(8,128)(2,1)} %emb_ref.1, f32[1,12288]{1,0:T(1,128)} %bitcast.3, bf16[384,384]{1,0:T(8,128)(2,1)} %wq_ref.1, bf16[2,512,384]{2,1,0:T(8,128)(2,1)} %key_ref.1, bf16[2,512,384]{2,1,0:T(8,128)(2,1)} %val_ref.1, ...), custom_call_target="tpu_custom_call" | custom-call | tf_op jit(solution)/shard_map/decode/pallas_call | solution.py:468
  97.3 1.4 %copy.11 = f32[64,96]{1,0:T(8,128)} copy(f32[64,96]{1,0:T(8,128)} %decode.1) | data formatting | bytes 49152

commit v3 on v2

--- a/solution.py
+++ b/solution.py
@@ -22,11 +22,11 @@
 def kernel(
     sizes,
     ids_ref, len_ref, emb_ref, lng_ref, wq_ref, key_ref, val_ref, wo_ref, fg_ref,
-    out_ref,
+    out_ref, lse_ref,
     emb, wq, key, val, wo,
-    p, r1, a1, a2, a3, b1, b2, b3, t0, r3, r4, r5, s1, s2, s3, s4,
+    p, r1, a1, a2, a3, b1, b2, b3, t0, r3, r4, r5, s1, sx, sy, s3, s4,
     part, rq, ra, att_all, op, ro1, ro2, gmat, dm, fb, fs, g1, g2,
-    load_sem, send_sem, recv_sem,
+    load_sem, send_sem, recv_sem, ring_sem,
 ):
     Y, Z, C, X, H = sizes
     NDP, XY, ZC, ZH = Y * Z * C, X * Y, Z * C, Z // 2
@@ -145,19 +145,27 @@
     def greet(dev):
         pl.semaphore_signal(barrier, inc=1, device_id=dev, device_id_type=MESH)
 
-    for kh in range(1, H):
-        for kz in range(Z):
-            greet({"mp_1": lax.rem(hi + kh, H), "dp_1": lax.rem(zi + kz, Z)})
-    each(NDP, lambda k: greet(dp_dev(lax.rem(dp + k, NDP))))
-    for kx in range(1, X):
-        for ky in range(Y):
-            for kc in range(C):
-                greet({
-                    "mp_0": lax.rem(xi + kx, X),
-                    "dp_0": lax.rem(yi + ky, Y),
-                    "dp_2": lax.rem(ci + kc, C),
-                })
-    greeted = NDP - 1 + (X - 1) * Y * C + (H - 1) * Z
+    ring = Z * H
+    greet(c_dev(1 - ci))
+    for own, n, dev in ((xi, X, x_dev), (yi, Y, y_dev), (zi, Z, z_dev)):
+        for k in range(1, n):
+            greet(dev(lax.rem(own + k, n)))
+    for k in (1, ring - 1):
+        greet(zz_dev(lax.rem(zz_own + k, ring)))
+    greeted = X + Y + Z
+    rounds = [d for d in (1, 2, 4, 8, 16) if 2 * d < ring]
+
+    def tell(r):
+        if r < len(rounds):
+            for k in (rounds[r], ring - rounds[r]):
+                pl.semaphore_signal(
+                    ring_sem.at[r], inc=1, device_id=zz_dev(lax.rem(zz_own + k, ring)),
+                    device_id_type=MESH,
+                )
+
+    def told(r):
+        if r < len(rounds):
+            pl.semaphore_wait(ring_sem.at[r], 2)
 
     flat = (dp * X + xi) * H + hi
     ids = ids_ref[...]
@@ -197,9 +205,12 @@
     acc = rows_of(acc, other, 0)
     pl.semaphore_wait(barrier, greeted)
     e1a = to_core(0)
+    tell(0)
     acc = rows_of(acc, other, 1)
     e1b = to_core(1)
     acc = rows_of(acc, ci, 0)
+    told(0)
+    tell(1)
     arrived(e1a, r1.at[0])
     summed(0)
     ea = exchange(lambda i: r1.at[0, :, i], a1.at[xi], xi, X, x_dev)
@@ -226,6 +237,8 @@
     var = jnp.concatenate(devs, axis=0)
     s1[ci] = to_rows((mean, var))[:8]
     es = gather(s1, ci, C, c_dev)
+    told(1)
+    tell(2)
 
     arrived(ea, a1.at[pl.ds(0, X - 1)])
     for yy in range(Y):
@@ -236,8 +249,8 @@
     ea = exchange(lambda i: a2.at[i], a3.at[yi], yi, Y, y_dev)
     a3[yi] = a2[yi]
     arrived(es, s1.at[pl.ds(0, C - 1)])
-    s2[xy] = jnp.sum(s1[...], axis=0)
-    es = gather(s2, xy, XY, xy_dev)
+    sx[xi] = jnp.sum(s1[...], axis=0)
+    es = gather(sx, xi, X, x_dev)
     arrived(eb, b1.at[pl.ds(0, Y - 1)])
     for xx in range(X):
         tot = b1[0, xx]
@@ -246,6 +259,9 @@
         b2[xx] = tot
     eb = exchange(lambda i: b2.at[i], b3.at[xi], xi, X, x_dev)
     b3[xi] = b2[xi]
+    arrived(es, sx.at[pl.ds(0, X - 1)])
+    sy[yi] = jnp.sum(sx[...], axis=0)
+    es = gather(sy, yi, Y, y_dev)
 
     half_row = lax.broadcasted_iota(jnp.int32, (16, W), 0)
     for j in range(NDP):
@@ -270,8 +286,8 @@
     t0[ZH:Z] = tot
     ez = exchange(lambda i: t0.at[i], r3.at[zi], zi, Z, z_dev)
     r3[zi] = t0[zi]
-    arrived(es, s2.at[pl.ds(0, XY - 1)])
-    s3[zi] = jnp.sum(s2[...], axis=0)
+    arrived(es, sy.at[pl.ds(0, Y - 1)])
+    s3[zi] = jnp.sum(sy[...], axis=0)
     es = gather(s3, zi, Z, z_dev)
 
     arrived(ez, r3.at[pl.ds(0, Z - 1)])
@@ -279,6 +295,7 @@
     for k in range(1, Z):
         tot = tot + r3[k]
     r4[hi] = tot
+    told(2)
     if H > 1:
         ez = gather(r4, hi, H, h_dev)
     arrived(es, s3.at[pl.ds(0, Z - 1)])
@@ -369,6 +386,29 @@
     eb = exchange(lambda i: fb.at[1, ci, :, yi], fb.at[1, ci, :, yi], yi, Y, y_dev)
     arrived(es, fs.at[ci, pl.ds(0, XY - 1)])
     es = exchange(lambda i: fs.at[ci], fs.at[ci], ci, C, c_dev)
+    arrived(es, fs.at[ci])
+    row_mean = jnp.zeros((1, 128), F32)
+    row_var = jnp.zeros((1, 128), F32)
+    blocks = []
+    for yy in range(Y):
+        for zz in range(Z):
+            for cc in range(C):
+                b = fs[cc, yy, zz]
+                for xx in range(1, X):
+                    b = b + fs[cc, xx * Y + yy, zz]
+                row_mean = row_mean + b[0:1]
+                row_var = row_var + b[1:2]
+                blocks.append(b[0:1])
+    row_mean = row_mean / NDP
+    for j in range(NDP):
+        off = blocks[j] - row_mean
+        row_var = row_var + W * (off * off)
+        dm[j : j + 1] = off
+    scale = to_cols((lax.rsqrt(row_var / D + EPS),))[:SEQ, 0:1]
+    offs = jnp.transpose(dm[...])[:SEQ, :NDP]
+    logits = jnp.dot(
+        offs, gmat[...], preferred_element_type=F32, precision=lax.Precision.HIGHEST
+    )
 
     def products(logits, core, half):
         for yy in range(Y):
@@ -392,34 +432,10 @@
             )
         return logits
 
-    logits = jnp.zeros((SEQ, V), F32)
     arrived(ea, fb.at[0, ci, pl.ds(0, X - 1)])
     ea = exchange(lambda i: fb.at[0, ci], fb.at[0, ci], ci, C, c_dev)
     arrived(eb, fb.at[1, ci, :, pl.ds(0, Y - 1)])
     eb = exchange(lambda i: fb.at[1, ci], fb.at[1, ci], ci, C, c_dev)
-    arrived(es, fs.at[ci])
-    row_mean = jnp.zeros((1, 128), F32)
-    row_var = jnp.zeros((1, 128), F32)
-    blocks = []
-    for yy in range(Y):
-        for zz in range(Z):
-            for cc in range(C):
-                b = fs[cc, yy, zz]
-                for xx in range(1, X):
-                    b = b + fs[cc, xx * Y + yy, zz]
-                row_mean = row_mean + b[0:1]
-                row_var = row_var + b[1:2]
-                blocks.append(b[0:1])
-    row_mean = row_mean / NDP
-    for j in range(NDP):
-        off = blocks[j] - row_mean
-        row_var = row_var + W * (off * off)
-        dm[j : j + 1] = off
-    scale = to_cols((lax.rsqrt(row_var / D + EPS),))[:SEQ, 0:1]
-    offs = jnp.transpose(dm[...])[:SEQ, :NDP]
-    logits = logits + jnp.dot(
-        offs, gmat[...], preferred_element_type=F32, precision=lax.Precision.HIGHEST
-    )
     logits = products(logits, ci, 0)
     logits = products(logits, ci, 1)
     arrived(ea, fb.at[0, other])
@@ -447,8 +463,9 @@
     eg = gather(g2, zz_own, Z * H, zz_dev)
     arrived(eg, g2.at[pl.ds(0, Z * H - 1)])
     best, tot = merged(g2)
-    stats = to_cols((best, jnp.log(tot)))
-    out_ref[...] = (logits - stats[:SEQ, 0:1]) - stats[:SEQ, 1:2]
+    stats = to_cols((best, jnp.log(tot)))[:SEQ]
+    out_ref[...] = logits - stats[:, 0:1]
+    lse_ref[...] = jnp.broadcast_to(stats[:, 1:2], (SEQ, V))
     for s, ref in pending:
         take(send_sem.at[s], ref)
 
@@ -465,12 +482,15 @@
     vmem = pl.BlockSpec(memory_space=pltpu.VMEM)
     smem = pl.BlockSpec(memory_space=pltpu.SMEM)
     hbm = pl.BlockSpec(memory_space=pl.ANY)
-    return pl.pallas_call(
+    logits, lse = pl.pallas_call(
         functools.partial(kernel, sizes),
         name="decode",
-        out_shape=jax.ShapeDtypeStruct((SEQ, V), F32),
+        out_shape=(
+            jax.ShapeDtypeStruct((SEQ, V), F32),
+            jax.ShapeDtypeStruct((SEQ, V), F32),
+        ),
         in_specs=[vmem, smem, hbm, vmem, hbm, hbm, hbm, hbm, vmem],
-        out_specs=vmem,
+        out_specs=(vmem, vmem),
         scratch_shapes=[
             pltpu.VMEM((V, D), BF16),
             pltpu.VMEM((W, HW), BF16),
@@ -490,7 +510,8 @@
             pltpu.VMEM((H, R, W), BF16),
             pltpu.VMEM((X, R, W), BF16),
             pltpu.VMEM((C, 8, 128), F32),
-            pltpu.VMEM((XY, 8, 128), F32),
+            pltpu.VMEM((X, 8, 128), F32),
+            pltpu.VMEM((Y, 8, 128), F32),
             pltpu.VMEM((Z, 8, 128), F32),
             pltpu.VMEM((H, 8, 128), F32),
             pltpu.VMEM((NDP, SP, HW), F32),
@@ -509,12 +530,14 @@
             pltpu.SemaphoreType.DMA((5,)),
             pltpu.SemaphoreType.DMA((NSEM,)),
             pltpu.SemaphoreType.DMA((NSEM,)),
+            pltpu.SemaphoreType.REGULAR((5,)),
         ],
         compiler_params=pltpu.CompilerParams(collective_id=0, has_side_effects=True),
     )(
         token_ids.reshape(1, -1), cache_lengths, embedding, ln_gain.reshape(1, -1), query_weight,
         key_cache, value_cache, out_weight, final_gain.reshape(1, -1),
     )
+    return logits - lse
 
 
 def solution(mesh, sizes=(4, 4, 2, 4, 4)):

time: 98.9 us -> 97 us (0.981)
  Pallas kernels: 97.3 us -> 95.3 us
  other arithmetic: 0 us -> 1.4 us
  local copies, waits for them, and re-layouts: 1.38 us -> 0 us
    pallas_call x1, Pallas kernels: 97.3 us -> 95.3 us  [per_device(): pl.pallas_call(functools.partial(kernel, sizes), name='decode', out_shape...]
    sub x0 -> x1, other arithmetic: none -> 1.4 us  [per_device(): return logits - lse]
    unnamed x1 -> x0, local copies, waits for them, and re-layouts: 1.38 us -> none
where the time goes in v3:
time: 97 us; the launch traced here: 96.7 us
  Pallas kernels  95.3 us (98%)
  other arithmetic  1.4 us (1%)
    pallas_call x1, Pallas kernels, per_device(): pl.pallas_call(functools.partial(kernel, sizes), name='decode', out_shape...  95.3 us

profile of v3, /device:TPU:1, one launch (start us, length us, event | category | flops | bytes accessed | tf_op | source)
XLA Modules:
  0.0 96.7 jit_solution(4064238366199054297)
XLA Ops:
  0.0 95.3 %decode.1 = (f32[64,96]{1,0:T(8,128)}, f32[64,96]{1,0:T(8,128)}) custom-call(s32[1,64]{1,0:T(1,128)} %bitcast.5, s32[2]{0:T(128)} %len_ref.1, bf16[96,12288]{1,0:T(8,128)(2,1)} %emb_ref.1, f32[1,12288]{1,0:T(1,128)} %bitcast.3, bf16[384,384]{1,0:T(8,128)(2,1)} %wq_ref.1, bf16[2,512,384]{2,1,0:T(8,128)(2,1)} %key_ref.1, bf16[2,512,384]{2,1,0:T(8,128)(2,1)} %val_ref.1, ...), custom_call_target="tpu_custom_call" | custom-call | tf_op jit(solution)/shard_map/decode/pallas_call | solution.py:485
  95.3 1.4 %sub.3 = f32[64,96]{1,0:T(8,128)} subtract(f32[64,96]{1,0:T(8,128)} %get-tuple-element.7, f32[64,96]{1,0:T(8,128)} %get-tuple-element.8) | non-fusion elementwise | flops 6144 | bytes 73728 | tf_op jit(solution)/shard_map/sub | solution.py:540

commit v4 on v3

--- a/solution.py
+++ b/solution.py
@@ -16,7 +16,7 @@
 MESH = pl.DeviceIdType.MESH
 F32 = jnp.float32
 BF16 = jnp.bfloat16
-NSEM = 36
+NSEM = 56
 
 
 def kernel(
@@ -131,12 +131,12 @@
             x = jnp.where(row == k, r, x)
         return jnp.transpose(x)
 
-    loads = [
-        pltpu.make_async_copy(a, b, load_sem.at[i])
-        for i, (a, b) in enumerate(
-            ((emb_ref, emb), (wq_ref, wq), (key_ref, key), (val_ref, val), (wo_ref, wo))
-        )
+    wide = Z * C * W
+    pairs = [
+        (emb_ref.at[:, pl.ds(k * wide, wide)], emb.at[:, pl.ds(k * wide, wide)]) for k in range(Y)
     ]
+    pairs += [(wq_ref, wq), (key_ref, key), (val_ref, val), (wo_ref, wo)]
+    loads = [pltpu.make_async_copy(a, b, load_sem.at[k]) for k, (a, b) in enumerate(pairs)]
     for c in loads:
         c.start()
 
@@ -175,51 +175,48 @@
     hot = jnp.where((row + flat * V == ids) & (row < V), 1.0, 0.0).astype(F32)
     hot = jnp.transpose(hot)[:SEQ, :V].astype(BF16)
 
-    loads[0].wait()
     other = 1 - ci
     acc = jnp.zeros((SEQ, 128), F32)
-
-    def rows_of(acc, core, half):
+    order = [half * ZH + k for k in range(ZH) for half in (0, 1)]
+
+    def rows_of(acc, core, zz, first):
         for yy in range(Y):
-            for zz in range(ZH):
-                b = (yy * Z + half * ZH + zz) * C + core
-                cols = pl.ds(pl.multiple_of(b * W, 128), W)
-                blk = jnp.dot(hot, emb[:, cols], preferred_element_type=F32)
-                for j in range(0, W, 128):
-                    acc = acc + blk[:, j : j + 128]
-                blk = blk.astype(BF16)
-                for xx in range(X):
-                    p[core, half, yy, xx, zz] = blk[xx * R : (xx + 1) * R]
+            if first:
+                loads[yy].wait()
+            b = (yy * Z + zz) * C + core
+            cols = pl.ds(pl.multiple_of(b * W, 128), W)
+            blk = jnp.dot(hot, emb[:, cols], preferred_element_type=F32)
+            for j in range(0, W, 128):
+                acc = acc + blk[:, j : j + 128]
+            blk = blk.astype(BF16)
+            for xx in range(X):
+                p[core, zz, yy, xx] = blk[xx * R : (xx + 1) * R]
         return acc
 
-    def to_core(half):
-        s = new()
-        send(s, p.at[other, half], r1.at[half], c_dev(other))
-        return s
-
-    def summed(half):
+    e1, ph = {}, {}
+    for n, zz in enumerate(order):
+        acc = rows_of(acc, other, zz, n == 0)
+        if n == 0:
+            pl.semaphore_wait(barrier, greeted)
+        e1[zz] = new()
+        send(e1[zz], p.at[other, zz], r1.at[zz], c_dev(other))
+        if n == 0:
+            tell(0)
+    for n, zz in enumerate(order):
+        acc = rows_of(acc, ci, zz, False)
+        arrived(e1[zz], r1.at[zz])
         for yy in range(Y):
             for xx in range(X):
-                r1[half, yy, xx] = r1[half, yy, xx] + p[ci, half, yy, xx]
-
-    acc = rows_of(acc, other, 0)
-    pl.semaphore_wait(barrier, greeted)
-    e1a = to_core(0)
-    tell(0)
-    acc = rows_of(acc, other, 1)
-    e1b = to_core(1)
-    acc = rows_of(acc, ci, 0)
-    told(0)
-    tell(1)
-    arrived(e1a, r1.at[0])
-    summed(0)
-    ea = exchange(lambda i: r1.at[0, :, i], a1.at[xi], xi, X, x_dev)
-    acc = rows_of(acc, ci, 1)
-    arrived(e1b, r1.at[1])
-    summed(1)
-    eb = exchange(lambda i: r1.at[1, i], b1.at[yi], yi, Y, y_dev)
-    a1[xi] = r1[0, :, xi]
-    b1[yi] = r1[1, yi]
+                r1[zz, yy, xx] = r1[zz, yy, xx] + p[ci, zz, yy, xx]
+        if zz < ZH:
+            ph[zz] = exchange(lambda i: r1.at[zz, :, i], a1.at[zz, xi], xi, X, x_dev)
+            a1[zz, xi] = r1[zz, :, xi]
+        else:
+            ph[zz] = exchange(lambda i: r1.at[zz, i], b1.at[zz - ZH, yi], yi, Y, y_dev)
+            b1[zz - ZH, yi] = r1[zz, yi]
+        if n == 0:
+            told(0)
+            tell(1)
 
     mean = jnp.sum(acc, axis=1, keepdims=True) / D
     devs = []
@@ -227,12 +224,11 @@
         m = mean[xx * R : (xx + 1) * R]
         sq = jnp.zeros((R, 128), F32)
         for cc in range(C):
-            for hh in range(2):
+            for zz in range(Z):
                 for yy in range(Y):
-                    for zz in range(ZH):
-                        d = p[cc, hh, yy, xx, zz].astype(F32) - m
-                        for j in range(0, W, 128):
-                            sq = sq + d[:, j : j + 128] * d[:, j : j + 128]
+                    d = p[cc, zz, yy, xx].astype(F32) - m
+                    for j in range(0, W, 128):
+                        sq = sq + d[:, j : j + 128] * d[:, j : j + 128]
         devs.append(jnp.sum(sq, axis=1, keepdims=True) / D)
     var = jnp.concatenate(devs, axis=0)
     s1[ci] = to_rows((mean, var))[:8]
@@ -240,25 +236,30 @@
     told(1)
     tell(2)
 
-    arrived(ea, a1.at[pl.ds(0, X - 1)])
-    for yy in range(Y):
-        tot = a1[0, yy]
-        for k in range(1, X):
-            tot = tot + a1[k, yy]
-        a2[yy] = tot
-    ea = exchange(lambda i: a2.at[i], a3.at[yi], yi, Y, y_dev)
-    a3[yi] = a2[yi]
-    arrived(es, s1.at[pl.ds(0, C - 1)])
-    sx[xi] = jnp.sum(s1[...], axis=0)
-    es = gather(sx, xi, X, x_dev)
-    arrived(eb, b1.at[pl.ds(0, Y - 1)])
-    for xx in range(X):
-        tot = b1[0, xx]
-        for k in range(1, Y):
-            tot = tot + b1[k, xx]
-        b2[xx] = tot
-    eb = exchange(lambda i: b2.at[i], b3.at[xi], xi, X, x_dev)
-    b3[xi] = b2[xi]
+    for n, zz in enumerate(order):
+        if zz < ZH:
+            arrived(ph[zz], a1.at[zz, pl.ds(0, X - 1)])
+            for yy in range(Y):
+                tot = a1[zz, 0, yy]
+                for k in range(1, X):
+                    tot = tot + a1[zz, k, yy]
+                a2[zz, yy] = tot
+            ph[zz] = exchange(lambda i: a2.at[zz, i], a3.at[zz, yi], yi, Y, y_dev)
+            a3[zz, yi] = a2[zz, yi]
+        else:
+            k0 = zz - ZH
+            arrived(ph[zz], b1.at[k0, pl.ds(0, Y - 1)])
+            for xx in range(X):
+                tot = b1[k0, 0, xx]
+                for k in range(1, Y):
+                    tot = tot + b1[k0, k, xx]
+                b2[k0, xx] = tot
+            ph[zz] = exchange(lambda i: b2.at[k0, i], b3.at[k0, xi], xi, X, x_dev)
+            b3[k0, xi] = b2[k0, xi]
+        if n == 0:
+            arrived(es, s1.at[pl.ds(0, C - 1)])
+            sx[xi] = jnp.sum(s1[...], axis=0)
+            es = gather(sx, xi, X, x_dev)
     arrived(es, sx.at[pl.ds(0, X - 1)])
     sy[yi] = jnp.sum(sx[...], axis=0)
     es = gather(sy, yi, Y, y_dev)
@@ -274,17 +275,22 @@
         )
         gmat[j : j + 1] = got[0:1] + got[1:2]
 
-    arrived(ea, a3.at[pl.ds(0, Y - 1)])
-    tot = a3[0]
-    for k in range(1, Y):
-        tot = tot + a3[k]
-    t0[0:ZH] = tot
-    arrived(eb, b3.at[pl.ds(0, X - 1)])
-    tot = b3[0]
-    for k in range(1, X):
-        tot = tot + b3[k]
-    t0[ZH:Z] = tot
-    ez = exchange(lambda i: t0.at[i], r3.at[zi], zi, Z, z_dev)
+    ez = new()
+    for zz in order:
+        if zz < ZH:
+            buf, cnt, k0 = a3, Y, zz
+        else:
+            buf, cnt, k0 = b3, X, zz - ZH
+        arrived(ph[zz], buf.at[k0, pl.ds(0, cnt - 1)])
+        tot = buf[k0, 0]
+        for k in range(1, cnt):
+            tot = tot + buf[k0, k]
+        t0[zz] = tot
+
+        @pl.when(zi != zz)
+        def _():
+            send(ez, t0.at[zz], r3.at[zi], z_dev(jnp.int32(zz)))
+
     r3[zi] = t0[zi]
     arrived(es, sy.at[pl.ds(0, Y - 1)])
     s3[zi] = jnp.sum(sy[...], axis=0)
@@ -318,14 +324,14 @@
     own_cols = pl.ds(pl.multiple_of(dp * W, 128), W)
     embedded = r5[...].reshape(SEQ, W).astype(F32)
     normed = (lng_ref[:, own_cols] * (embedded - mean) * lax.rsqrt(var + EPS)).astype(BF16)
-    loads[1].wait()
+    loads[Y].wait()
     partial = jnp.dot(normed, wq[...], preferred_element_type=F32)
     for j in range(NDP):
         part[j] = partial[j * SP : (j + 1) * SP]
     eq = exchange(lambda i: part.at[i], rq.at[dp], dp, NDP, dp_dev)
     rq[dp] = part[dp]
-    loads[2].wait()
-    loads[3].wait()
+    loads[Y + 1].wait()
+    loads[Y + 2].wait()
     arrived(eq, rq.at[pl.ds(0, NDP - 1)])
     queries = (jnp.sum(rq[...], axis=0) * HD**-0.5).astype(BF16).astype(F32)
 
@@ -346,12 +352,12 @@
         got = jnp.dot(w, val[s], preferred_element_type=F32)
         got = jnp.sum(jnp.where(own_head, got, 0.0), axis=0, keepdims=True)
         attended = jnp.where(pair == s, got, attended)
-    ra[dp] = attended.astype(BF16).astype(F32)
+    ra[dp] = attended.astype(BF16)
     eg = gather(ra, dp, NDP, dp_dev)
-    loads[4].wait()
+    loads[Y + 3].wait()
     arrived(eg, ra.at[pl.ds(0, NDP - 1)])
     for j in range(NDP):
-        att_all[j * SP : (j + 1) * SP] = ra[j]
+        att_all[j * SP : (j + 1) * SP] = ra[j].astype(F32)
 
     mixed = jnp.dot(att_all[...].astype(BF16), wo[...], preferred_element_type=F32)
     for xx in range(X):
@@ -367,23 +373,27 @@
 
     m = jnp.sum(hidden, axis=1, keepdims=True) / W
     d = hidden - m
-    zh, zl = lax.div(zi, ZH), lax.rem(zi, ZH)
-    fb[zh, ci, xi, yi, zl] = (fg_ref[:, own_cols] * d).astype(BF16)
-    ef = exchange(
-        lambda i: fb.at[zh, ci, xi, yi, zl], fb.at[zh, ci, xi, yi, zl], zi, Z, z_dev
-    )
+    fb[zi, ci, xi, yi] = (fg_ref[:, own_cols] * d).astype(BF16)
+    ef = exchange(lambda i: fb.at[zi, ci, xi, yi], fb.at[zi, ci, xi, yi], zi, Z, z_dev)
     fs[ci, xy, zi] = to_rows((m, jnp.sum(d * d, axis=1, keepdims=True)), xi * R)[:2]
     es = exchange(lambda i: fs.at[ci, xy, zi], fs.at[ci, xy, zi], zi, Z, z_dev)
 
-    arrived(ef, fb.at[0, 0, 0, pl.ds(0, Z - 1), 0])
-    ea = exchange(lambda i: fb.at[0, ci, xi, yi], fb.at[0, ci, xi, yi], yi, Y, y_dev)
-    eb = exchange(lambda i: fb.at[1, ci, xi, yi], fb.at[1, ci, xi, yi], xi, X, x_dev)
+    arrived(ef, fb.at[pl.ds(0, Z - 1), 0, 0, 0])
+    for zz in order:
+        own = fb.at[zz, ci, xi, yi]
+        own_n_dev = (yi, Y, y_dev) if zz < ZH else (xi, X, x_dev)
+        ph[zz] = exchange(lambda i: own, own, *own_n_dev)
     arrived(es, fs.at[ci, xy, pl.ds(0, Z - 1)])
     es = exchange(lambda i: fs.at[ci, xy], fs.at[ci, xy], xy, XY, xy_dev)
-    arrived(ea, fb.at[0, ci, xi, pl.ds(0, Y - 1)])
-    ea = exchange(lambda i: fb.at[0, ci, xi], fb.at[0, ci, xi], xi, X, x_dev)
-    arrived(eb, fb.at[1, ci, pl.ds(0, X - 1), yi])
-    eb = exchange(lambda i: fb.at[1, ci, :, yi], fb.at[1, ci, :, yi], yi, Y, y_dev)
+    for zz in order:
+        if zz < ZH:
+            arrived(ph[zz], fb.at[zz, ci, xi, pl.ds(0, Y - 1)])
+            own = fb.at[zz, ci, xi]
+            ph[zz] = exchange(lambda i: own, own, xi, X, x_dev)
+        else:
+            arrived(ph[zz], fb.at[zz, ci, pl.ds(0, X - 1), yi])
+            own = fb.at[zz, ci, :, yi]
+            ph[zz] = exchange(lambda i: own, own, yi, Y, y_dev)
     arrived(es, fs.at[ci, pl.ds(0, XY - 1)])
     es = exchange(lambda i: fs.at[ci], fs.at[ci], ci, C, c_dev)
     arrived(es, fs.at[ci])
@@ -410,38 +420,32 @@
         offs, gmat[...], preferred_element_type=F32, precision=lax.Precision.HIGHEST
     )
 
-    def products(logits, core, half):
+    def products(logits, zz):
+        arrived(ph[zz], fb.at[zz, other])
         for yy in range(Y):
             lhs = jnp.concatenate(
                 [
-                    jnp.concatenate([fb[half, core, xx, yy, zz] for xx in range(X)], axis=0)
-                    for zz in range(ZH)
+                    jnp.concatenate([fb[zz, cc, xx, yy] for xx in range(X)], axis=0)
+                    for cc in range(C)
                 ],
                 axis=1,
             )
-            rhs = jnp.concatenate(
-                [
-                    emb[:, pl.ds(pl.multiple_of(
-                        ((yy * Z + half * ZH + zz) * C + core) * W, 128), W)]
-                    for zz in range(ZH)
-                ],
-                axis=1,
-            )
+            b = (yy * Z + zz) * C * W
             logits = logits + lax.dot_general(
-                lhs, rhs, (((1,), (1,)), ((), ())), preferred_element_type=F32
+                lhs, emb[:, b : b + C * W], (((1,), (1,)), ((), ())), preferred_element_type=F32
             )
         return logits
 
-    arrived(ea, fb.at[0, ci, pl.ds(0, X - 1)])
-    ea = exchange(lambda i: fb.at[0, ci], fb.at[0, ci], ci, C, c_dev)
-    arrived(eb, fb.at[1, ci, :, pl.ds(0, Y - 1)])
-    eb = exchange(lambda i: fb.at[1, ci], fb.at[1, ci], ci, C, c_dev)
-    logits = products(logits, ci, 0)
-    logits = products(logits, ci, 1)
-    arrived(ea, fb.at[0, other])
-    logits = products(logits, other, 0)
-    arrived(eb, fb.at[1, other])
-    logits = products(logits, other, 1) * scale
+    for n, zz in enumerate(order):
+        if zz < ZH:
+            arrived(ph[zz], fb.at[zz, ci, pl.ds(0, X - 1)])
+        else:
+            arrived(ph[zz], fb.at[zz, ci, :, pl.ds(0, Y - 1)])
+        own = fb.at[zz, ci]
+        ph[zz] = exchange(lambda i: own, own, ci, C, c_dev)
+        if n > 0:
+            logits = products(logits, order[n - 1])
+    logits = products(logits, order[-1]) * scale
 
     top = jnp.max(logits, axis=1, keepdims=True)
     total = jnp.sum(jnp.exp(logits - top), axis=1, keepdims=True)
@@ -497,14 +501,14 @@
             pltpu.VMEM((SP, T, HW), BF16),
             pltpu.VMEM((SP, T, HW), BF16),
             pltpu.VMEM((HW, W), BF16),
-            pltpu.VMEM((C, 2, Y, X, ZH, R, W), BF16),
-            pltpu.VMEM((2, Y, X, ZH, R, W), BF16),
-            pltpu.VMEM((X, Y, ZH, R, W), BF16),
-            pltpu.VMEM((Y, ZH, R, W), BF16),
-            pltpu.VMEM((Y, ZH, R, W), BF16),
-            pltpu.VMEM((Y, X, ZH, R, W), BF16),
-            pltpu.VMEM((X, ZH, R, W), BF16),
-            pltpu.VMEM((X, ZH, R, W), BF16),
+            pltpu.VMEM((C, Z, Y, X, R, W), BF16),
+            pltpu.VMEM((Z, Y, X, R, W), BF16),
+            pltpu.VMEM((ZH, X, Y, R, W), BF16),
+            pltpu.VMEM((ZH, Y, R, W), BF16),
+            pltpu.VMEM((ZH, Y, R, W), BF16),
+            pltpu.VMEM((ZH, Y, X, R, W), BF16),
+            pltpu.VMEM((ZH, X, R, W), BF16),
+            pltpu.VMEM((ZH, X, R, W), BF16),
             pltpu.VMEM((Z, R, W), BF16),
             pltpu.VMEM((Z, R, W), BF16),
             pltpu.VMEM((H, R, W), BF16),
@@ -516,18 +520,18 @@
             pltpu.VMEM((H, 8, 128), F32),
             pltpu.VMEM((NDP, SP, HW), F32),
             pltpu.VMEM((NDP, SP, HW), F32),
-            pltpu.VMEM((NDP, SP, HW), F32),
+            pltpu.VMEM((NDP, SP, HW), BF16),
             pltpu.VMEM((SEQ, HW), F32),
             pltpu.VMEM((X, R, W), F32),
             pltpu.VMEM((X, R, W), F32),
             pltpu.VMEM((H, R, W), BF16),
             pltpu.VMEM((NDP, V), F32),
             pltpu.VMEM((max(NDP, 128), 128), F32),
-            pltpu.VMEM((2, C, X, Y, ZH, R, W), BF16),
+            pltpu.VMEM((Z, C, X, Y, R, W), BF16),
             pltpu.VMEM((C, XY, Z, 2, 128), F32),
             pltpu.VMEM((XY * C, 2, 128), F32),
             pltpu.VMEM((Z * H, 2, 128), F32),
-            pltpu.SemaphoreType.DMA((5,)),
+            pltpu.SemaphoreType.DMA((Y + 4,)),
             pltpu.SemaphoreType.DMA((NSEM,)),
             pltpu.SemaphoreType.DMA((NSEM,)),
             pltpu.SemaphoreType.REGULAR((5,)),

time: 97 us -> 95.8 us (0.988)
  Pallas kernels: 95.3 us -> 94.2 us
    pallas_call x1, Pallas kernels: 95.3 us -> 94.2 us  [per_device(): pl.pallas_call(functools.partial(kernel, sizes), name='decode', out_shape...]
where the time goes in v4:
time: 95.8 us; the launch traced here: 95.6 us
  Pallas kernels  94.2 us (98%)
  other arithmetic  1.4 us (1%)
    pallas_call x1, Pallas kernels, per_device(): pl.pallas_call(functools.partial(kernel, sizes), name='decode', out_shape...  94.2 us

profile of v4, /device:TPU:1, one launch (start us, length us, event | category | flops | bytes accessed | tf_op | source)
XLA Modules:
  0.0 95.6 jit_solution(16613489828584009034)
XLA Ops:
  0.0 94.2 %decode.1 = (f32[64,96]{1,0:T(8,128)}, f32[64,96]{1,0:T(8,128)}) custom-call(s32[1,64]{1,0:T(1,128)} %bitcast.5, s32[2]{0:T(128)} %len_ref.1, bf16[96,12288]{1,0:T(8,128)(2,1)} %emb_ref.1, f32[1,12288]{1,0:T(1,128)} %bitcast.3, bf16[384,384]{1,0:T(8,128)(2,1)} %wq_ref.1, bf16[2,512,384]{2,1,0:T(8,128)(2,1)} %key_ref.1, bf16[2,512,384]{2,1,0:T(8,128)(2,1)} %val_ref.1, ...), custom_call_target="tpu_custom_call" | custom-call | tf_op jit(solution)/shard_map/decode/pallas_call | solution.py:489
  94.2 1.4 %sub.3 = f32[64,96]{1,0:T(8,128)} subtract(f32[64,96]{1,0:T(8,128)} %get-tuple-element.7, f32[64,96]{1,0:T(8,128)} %get-tuple-element.8) | non-fusion elementwise | flops 6144 | bytes 73728 | tf_op jit(solution)/shard_map/sub | solution.py:544

commit v5 on v4

--- a/solution.py
+++ b/solution.py
@@ -25,7 +25,7 @@
     out_ref, lse_ref,
     emb, wq, key, val, wo,
     p, r1, a1, a2, a3, b1, b2, b3, t0, r3, r4, r5, s1, sx, sy, s3, s4,
-    part, rq, ra, att_all, op, ro1, ro2, gmat, dm, fb, fs, g1, g2,
+    part, rq, mine, ra, att_all, ro2, gmat, dm, fb, fs, g1, g2,
     load_sem, send_sem, recv_sem, ring_sem,
 ):
     Y, Z, C, X, H = sizes
@@ -41,6 +41,7 @@
     xy = xi * Y + yi
     zz_own = hi * Z + zi
     xyc = xy * C + ci
+    zc = zi * C + ci
     dp = (yi * Z + zi) * C + ci
 
     def xy_dev(i):
@@ -135,7 +136,7 @@
     pairs = [
         (emb_ref.at[:, pl.ds(k * wide, wide)], emb.at[:, pl.ds(k * wide, wide)]) for k in range(Y)
     ]
-    pairs += [(wq_ref, wq), (key_ref, key), (val_ref, val), (wo_ref, wo)]
+    pairs += [(wq_ref, wq), (key_ref, key), (val_ref, val), (wo_ref, wo.at[xi])]
     loads = [pltpu.make_async_copy(a, b, load_sem.at[k]) for k, (a, b) in enumerate(pairs)]
     for c in loads:
         c.start()
@@ -263,6 +264,15 @@
     arrived(es, sx.at[pl.ds(0, X - 1)])
     sy[yi] = jnp.sum(sx[...], axis=0)
     es = gather(sy, yi, Y, y_dev)
+    loads[Y + 3].wait()
+    ew = new()
+
+    def to_x(k):
+        send(ew, wo.at[xi], wo.at[xi], x_dev(lax.rem(xi + k, X)))
+
+    for k in range(1, X):
+        if 2 * k != X:
+            to_x(k)
 
     half_row = lax.broadcasted_iota(jnp.int32, (16, W), 0)
     for j in range(NDP):
@@ -314,6 +324,7 @@
         tot = tot + r4[k]
     r5[xi] = tot
     ex = gather(r5, xi, X, x_dev)
+    to_x(X // 2)
     if H > 1:
         arrived(es, s4.at[pl.ds(0, H - 1)])
     stats = jnp.sum(s4[...], axis=0)
@@ -352,20 +363,41 @@
         got = jnp.dot(w, val[s], preferred_element_type=F32)
         got = jnp.sum(jnp.where(own_head, got, 0.0), axis=0, keepdims=True)
         attended = jnp.where(pair == s, got, attended)
-    ra[dp] = attended.astype(BF16)
-    eg = gather(ra, dp, NDP, dp_dev)
-    loads[Y + 3].wait()
-    arrived(eg, ra.at[pl.ds(0, NDP - 1)])
-    for j in range(NDP):
-        att_all[j * SP : (j + 1) * SP] = ra[j].astype(F32)
-
-    mixed = jnp.dot(att_all[...].astype(BF16), wo[...], preferred_element_type=F32)
+    mine[...] = attended.astype(BF16)
+    slot = xi * ZC + zc
+    et = new()
+
+    def to_quarter(i):
+        send(et, mine, ra.at[slot], {**dp_dev(i), "mp_0": yi})
+
+    each(NDP, lambda k: to_quarter(lax.rem(dp + k, NDP)))
+
+    @pl.when(xi != yi)
+    def _():
+        to_quarter(dp)
+
+    @pl.when(xi == yi)
+    def _():
+        ra[slot] = mine[...]
+
+    def attended_waits(sem):
+        @pl.when(xi != yi)
+        def _():
+            take(sem, ra)
+
+        @pl.when(xi == yi)
+        def _():
+            take(sem, ra.at[pl.ds(0, X * ZC - 1)])
+
+    arrived(ew, wo.at[pl.ds(0, X - 1)])
+    attended_waits(recv_sem.at[et])
     for xx in range(X):
-        op[xx] = mixed[xx * R : (xx + 1) * R]
-    eo = exchange(lambda i: op.at[i], ro1.at[xi], xi, X, x_dev)
-    ro1[xi] = op[xi]
-    arrived(eo, ro1.at[pl.ds(0, X - 1)])
-    ro2[hi] = jnp.sum(ro1[...], axis=0).astype(BF16)
+        for j in range(ZC):
+            att_all[j * SP : (j + 1) * SP, xx * HW : (xx + 1) * HW] = ra[xx * ZC + j].astype(F32)
+    mixed = jnp.dot(
+        att_all[...].astype(BF16), wo[...].reshape(X * HW, W), preferred_element_type=F32
+    )
+    ro2[hi] = mixed.astype(BF16)
     if H > 1:
         eo = gather(ro2, hi, H, h_dev)
         arrived(eo, ro2.at[pl.ds(0, H - 1)])
@@ -470,6 +502,7 @@
     stats = to_cols((best, jnp.log(tot)))[:SEQ]
     out_ref[...] = logits - stats[:, 0:1]
     lse_ref[...] = jnp.broadcast_to(stats[:, 1:2], (SEQ, V))
+    attended_waits(send_sem.at[et])
     for s, ref in pending:
         take(send_sem.at[s], ref)
 
@@ -500,7 +533,7 @@
             pltpu.VMEM((W, HW), BF16),
             pltpu.VMEM((SP, T, HW), BF16),
             pltpu.VMEM((SP, T, HW), BF16),
-            pltpu.VMEM((HW, W), BF16),
+            pltpu.VMEM((X, HW, W), BF16),
             pltpu.VMEM((C, Z, Y, X, R, W), BF16),
             pltpu.VMEM((Z, Y, X, R, W), BF16),
             pltpu.VMEM((ZH, X, Y, R, W), BF16),
@@ -520,10 +553,9 @@
             pltpu.VMEM((H, 8, 128), F32),
             pltpu.VMEM((NDP, SP, HW), F32),
             pltpu.VMEM((NDP, SP, HW), F32),
-            pltpu.VMEM((NDP, SP, HW), BF16),
-            pltpu.VMEM((SEQ, HW), F32),
-            pltpu.VMEM((X, R, W), F32),
-            pltpu.VMEM((X, R, W), F32),
+            pltpu.VMEM((SP, HW), BF16),
+            pltpu.VMEM((X * Z * C, SP, HW), BF16),
+            pltpu.VMEM((R, X * HW), F32),
             pltpu.VMEM((H, R, W), BF16),
             pltpu.VMEM((NDP, V), F32),
             pltpu.VMEM((max(NDP, 128), 128), F32),

time: 95.8 us -> 95.3 us (level)
  no operation moved by 1% of the time
where the time goes in v5:
time: 95.3 us; the launch traced here: 95.1 us
  Pallas kernels  93.7 us (98%)
  other arithmetic  1.4 us (1%)
    pallas_call x1, Pallas kernels, per_device(): pl.pallas_call(functools.partial(kernel, sizes), name='decode', out_shape...  93.7 us

profile of v5, /device:TPU:1, one launch (start us, length us, event | category | flops | bytes accessed | tf_op | source)
XLA Modules:
  0.0 95.1 jit_solution(13205481900593940375)
XLA Ops:
  0.0 93.7 %decode.1 = (f32[64,96]{1,0:T(8,128)}, f32[64,96]{1,0:T(8,128)}) custom-call(s32[1,64]{1,0:T(1,128)} %bitcast.5, s32[2]{0:T(128)} %len_ref.1, bf16[96,12288]{1,0:T(8,128)(2,1)} %emb_ref.1, f32[1,12288]{1,0:T(1,128)} %bitcast.3, bf16[384,384]{1,0:T(8,128)(2,1)} %wq_ref.1, bf16[2,512,384]{2,1,0:T(8,128)(2,1)} %key_ref.1, bf16[2,512,384]{2,1,0:T(8,128)(2,1)} %val_ref.1, ...), custom_call_target="tpu_custom_call" | custom-call | tf_op jit(solution)/shard_map/decode/pallas_call | solution.py:522
  93.7 1.4 %sub.3 = f32[64,96]{1,0:T(8,128)} subtract(f32[64,96]{1,0:T(8,128)} %get-tuple-element.7, f32[64,96]{1,0:T(8,128)} %get-tuple-element.8) | non-fusion elementwise | flops 6144 | bytes 73728 | tf_op jit(solution)/shard_map/sub | solution.py:576
